TPU v7x, 128 devices: a whole 4x4x4 slice. The times are simulated.
128 devices in a mesh: section: 4 (over z), shard: 32 (over y, x, core).
Axes of the slice: x: 4, y: 4, z: 4, core: 2. Of those that a mesh axis runs over, the one named last changes fastest.
Arguments:
- grad_parts: bfloat16 [4, 32, 1024, 8192], P('section', 'shard'), may hold values from -6 to 6
- params: bfloat16 [4, 1024, 8192], P('section', 'shard'), may hold values from -6 to 6
- moment_first: float32 [4, 1024, 8192], P('section', 'shard'), may hold values from -6 to 6
- moment_second: float32 [4, 1024, 8192], P('section', 'shard'), may hold values from 0.5 to 50
- block_layer: int32 [4, 128], P('section', 'shard'), may hold values from 0 to 7, as said below
- block_valid: int32 [4, 128], P('section', 'shard'), may hold values from 0 to 1
- decay: float32 [8], replicated, may hold values from 0.05 to 1
Outputs:
- new_params: bfloat16 [4, 1024, 8192], P('section', 'shard')
- new_first: float32 [4, 1024, 8192], P('section', 'shard')
- new_second: float32 [4, 1024, 8192], P('section', 'shard')
- ratios: float32 [8], replicated
Inputs may be any that keep to these rules, and one draw needn't show every extreme that they name: `block_layer`: in every section the live slots come first. One section has all 128 slots live; each other section has between 64 and 128 live slots, and all sections together have 3 * 128. Over the live slots taken section by section in order, layer ids never fall and every layer has exactly 48 live slots; dead slots hold arbitrary layer ids.
All inputs are finite; a program needn't handle non-finite values.
Results may differ from a plain program's by a relative error of at most 0.008.
Values may be sent and summed in bfloat16 or wider, within the bound.
A program may use at most 64 MiB of HBM per device.

v0:
```python
import jax
import jax.numpy as jnp
from jax import lax
from jax.sharding import PartitionSpec as P

bias_first = 1.0 - 0.9**10
bias_second = 1.0 - 0.99**10


def from_everyone(x, axis):
    length = lax.axis_size(axis)
    return lax.all_to_all(jnp.broadcast_to(x[None], (length, *x.shape)), axis, 0, 0, tiled=True)


def taken_together(x, axis):
    return from_everyone(x, axis).sum(axis=0)


def carried_in(part, axis, combine, identity):
    place = lax.axis_index(axis)
    gathered = lax.all_gather(part, axis)
    state = jnp.zeros_like(part) + jnp.asarray(identity, part.dtype)

    def one(step, state):
        return combine(state, lax.dynamic_index_in_dim(gathered, step, 0, False))

    return lax.fori_loop(0, place, one, state)


def broadcast(x, axis, root):
    return lax.dynamic_index_in_dim(lax.all_gather(x, axis), root, 0, keepdims=False)


def combine_sum(earlier, later):
    return earlier + later


def shards(grad_parts, params, moment_first, moment_second, block_layer, block_valid, decay):
    row_count = params.shape[1]
    local_grad = grad_parts[0, 0]
    gradient = lax.psum_scatter(
        local_grad.astype(jnp.float32).astype(jnp.bfloat16),
        "shard",
        scatter_dimension=0,
        tiled=True,
    ).astype(jnp.float32)
    block_rows = row_count // block_layer.shape[1]
    layer_rows = jnp.repeat(block_layer[0], block_rows)
    valid_rows = jnp.repeat(block_valid[0], block_rows) > 0
    layer_ids = jnp.arange(decay.shape[0], dtype=jnp.int32)
    onehot = jnp.where(
        valid_rows[:, None] & (layer_rows[:, None] == layer_ids[None, :]), 1.0, 0.0
    ).astype(jnp.float32)
    weights = params[0].astype(jnp.float32)
    first = 0.9 * moment_first[0] + 0.1 * gradient
    second = 0.99 * moment_second[0] + 0.01 * gradient * gradient
    row_decay = jnp.dot(onehot, decay)
    update = (
        first / bias_first / (jnp.sqrt(second / bias_second) + 1e-06) + row_decay[:, None] * weights
    )
    row_sums = jnp.stack(
        [jnp.sum(weights * weights, axis=-1), jnp.sum(update * update, axis=-1)], axis=1
    )
    partial_value = jnp.dot(onehot.T, row_sums)
    section_total = taken_together(partial_value, "shard")
    before = carried_in(section_total, "section", combine_sum, jnp.zeros_like(section_total))
    through = before + section_total
    totals = broadcast(through, "section", lax.axis_size("section") - 1)
    ratios = jnp.sqrt(totals[:, 0] / (totals[:, 1] + 1.0))
    row_ratio = jnp.dot(onehot, ratios)
    stepped = weights - 0.1 * row_ratio[:, None] * update
    live = valid_rows[:, None]
    new_params = jnp.where(live, stepped, weights).astype(jnp.bfloat16)
    new_first = jnp.where(live, first, moment_first[0])
    new_second = jnp.where(live, second, moment_second[0])
    return (new_params[None], new_first[None], new_second[None], ratios)


def solution(mesh):
    placed = (
        P("section", "shard", None, None),
        P("section", "shard", None),
        P("section", "shard", None),
        P("section", "shard", None),
        P("section", "shard"),
        P("section", "shard"),
        P(),
    )
    return jax.shard_map(
        shards,
        mesh=mesh,
        in_specs=placed,
        out_specs=(
            P("section", "shard", None),
            P("section", "shard", None),
            P("section", "shard", None),
            P(),
        ),
        check_vma=False,
    )
```

profile of v0, /device:TPU:1, one launch (start us, length us, event | category | flops | bytes accessed | tf_op | source)
XLA Modules:
  0.0 169.9 jit_solution(13518793935632304975)
XLA Ops:
  7.2 0.0 copy-start
  7.2 0.0 copy-start.4
  7.2 0.0 copy-start.3
  7.2 0.0 copy-start.1
  7.2 0.0 copy-start.2
  7.2 0.0 reduce-scatter.2.cloned.1.call-start
  7.3 0.7 reduce-scatter.2.cloned.1.call-update
  8.0 0.0 copy-done.4
  8.0 0.1 broadcast_in_dim.48
  8.1 0.1 gt.20
  8.1 0.0 copy-done.3
  8.1 0.1 broadcast_in_dim.50
  8.2 0.1 eq.15
  8.3 0.0 copy-done
  8.3 0.2 convolution_bitcast_fusion.1
  8.5 120.5 %reduce-scatter.2.cloned.1.call-done = bf16[32,8192]{1,0:T(8,128)(2,1)} async-done(((bf16[1024,8192]{1,0:T(8,128)(2,1)}), bf16[32,8192]{1,0:T(8,128)(2,1)}) %reduce-scatter.2.cloned.1.call-update) | async-done | bytes 524304 | tf_op jit(solution)/shard_map/reduce_scatter | solution.py:41
  129.0 0.0 copy-done.1
  129.0 0.0 copy-done.2
  129.0 3.8 %multiply_reduce_fusion = (bf16[32]{0:T(256)(128)(2,1)S(1)}, f32[32,8192]{1,0:T(8,128)S(1)}, f32[1,32,8192]{2,1,0:T(8,128)}, f32[1,32,8192]{2,1,0:T(8,128)}, bf16[32]{0:T(256)(128)(2,1)S(1)}) fusion(bf16[1,32,8192]{2,1,0:T(8,128)(2,1)S(1)} %copy-done.1, f32[32]{0:T(128)S(1)} %convolution_bitcast_fusion.1, f32[1,32,8192]{2,1,0:T(8,128)S(1)} %copy-done.2, ...), kind=kLoop, calls=%fused_computation.26 | loop fusion | flops 5504960 | bytes 6291744 | tf_op jit(solution)/shard_map/reduce_sum | solution.py:62
  132.8 0.2 fusion.15
  133.0 0.6 broadcast_in_dim.53
  133.7 7.0 %all-to-all-start = ((f32[32,8,2]{1,2,0:T(2,128)}), f32[32,8,2]{1,2,0:T(2,128)S(1)}, u32[]{:S(2)}, u32[]{:S(2)}) async-start(f32[32,8,2]{1,2,0:T(2,128)} %broadcast_in_dim.53), calls=%async_computation.1 | async-start | bytes 65536 | tf_op jit(solution)/shard_map/all_to_all | solution.py:12
  140.7 7.3 %all-to-all-done = f32[32,8,2]{1,2,0:T(2,128)S(1)} async-done(((f32[32,8,2]{1,2,0:T(2,128)}), f32[32,8,2]{1,2,0:T(2,128)S(1)}, u32[]{:S(2)}, u32[]{:S(2)}) %all-to-all-start) | async-done | bytes 2080 | tf_op jit(solution)/shard_map/all_to_all | solution.py:12
  148.0 7.9 %all-gather.2 = f32[4,8,2]{1,2,0:T(2,128)S(1)} all-gather(f32[1,8,2]{1,2,0:T(2,128)S(1)} %bitcast.83), channel_id=2, replica_groups=mesh['section'=4,'shard'=32] {'section'}, dimensions={0}, use_global_device_ids=true | all-gather | bytes 320 | tf_op jit(solution)/shard_map/all_gather | solution.py:21
  155.9 5.2 %all-gather.3 = f32[4,8,2]{1,2,0:T(2,128)S(1)} all-gather(f32[1,8,2]{1,2,0:T(2,128)S(1)} %add_bitcast_fusion), channel_id=3, replica_groups=mesh['section'=4,'shard'=32] {'section'}, dimensions={0}, use_global_device_ids=true | all-gather | bytes 320 | tf_op jit(solution)/shard_map/all_gather | solution.py:31
  161.2 0.1 reshape.37
  161.3 0.2 fusion
  161.5 0.6 fusion.52
  162.1 1.0 fusion.13
  (6 shorter events, 0.1 us)
Async XLA Ops:
  7.2 1.1 copy-start
  7.2 0.8 copy-start.4
  7.2 1.0 copy-start.3
  7.2 121.8 %copy-start.1 = (bf16[1,32,8192]{2,1,0:T(8,128)(2,1)S(1)}, bf16[1,32,8192]{2,1,0:T(8,128)(2,1)}, u32[]{:S(2)}) copy-start(bf16[1,32,8192]{2,1,0:T(8,128)(2,1)} %param.10) | copy-start | bytes 1572868
  7.2 121.8 %copy-start.2 = (f32[1,32,8192]{2,1,0:T(8,128)S(1)}, f32[1,32,8192]{2,1,0:T(8,128)}, u32[]{:S(2)}) copy-start(f32[1,32,8192]{2,1,0:T(8,128)} %param.12) | copy-start | bytes 3145732
  7.2 121.8 %reduce-scatter.2.cloned.1.call-start = ((), (), s32[]{:S(2)}) async-start(), calls=%async_computation.2 | async-start | bytes 17301504 | tf_op jit(solution)/shard_map/reduce_scatter | solution.py:41
  133.7 14.3 %all-to-all-start = ((f32[32,8,2]{1,2,0:T(2,128)}), f32[32,8,2]{1,2,0:T(2,128)S(1)}, u32[]{:S(2)}, u32[]{:S(2)}) async-start(f32[32,8,2]{1,2,0:T(2,128)} %broadcast_in_dim.53), calls=%async_computation.1 | async-start | bytes 65536 | tf_op jit(solution)/shard_map/all_to_all | solution.py:12
Sparse Core Ops, SparseCore 0:
  11.9 117.0 reduce-scatter.1
where the time goes:
time: 173 us; the launch traced here: 170 us
  waiting for transfers between devices  128 us (74%)
  between operations  14.1 us (8%)
  blocking collectives  13.1 us (8%)
  starting transfers between devices  7.07 us (4%)
  other arithmetic  5.5 us (3%)
    reduce_scatter x1, waiting for transfers between devices, shards(): lax.psum_scatter(local_grad.astype(jnp.float32).astype(jnp.bfloat16), 'sh...  121 us
    all_gather x1, blocking collectives, carried_in(): gathered = lax.all_gather(part, axis)  7.89 us
    all_to_all x1, waiting for transfers between devices, from_everyone(): lax.all_to_all(jnp.broadcast_to(x[None], (length, *x.shape)), axis, 0, 0,...  7.25 us
    all_to_all x1, starting transfers between devices, from_everyone(): lax.all_to_all(jnp.broadcast_to(x[None], (length, *x.shape)), axis, 0, 0,...  7.04 us
    all_gather x1, blocking collectives, broadcast(): lax.all_gather(x, axis)  5.24 us
    reduce_sum x1, other arithmetic, shards(): jnp.sum(update * update, axis=-1)  3.8 us
  transfers between devices with their start and end apart: 2, of which 2 were waited for; matrix products, arithmetic and copies ran while one was open for 0% of the time, Pallas kernels for 0%

commit v1 on v0

v1 whole, which is shorter than its diff:
```python
import functools

import jax
import jax.numpy as jnp
from jax import lax
from jax.experimental import pallas as pl
from jax.experimental.pallas import tpu as pltpu
from jax.sharding import PartitionSpec as P

bias_first = 1.0 - 0.9**10
bias_second = 1.0 - 0.99**10

MESH = pl.DeviceIdType.MESH
F32, BF16 = jnp.float32, jnp.bfloat16
SIDE = 4
ORDER = (2, 1, 3, 0)
FAR, NEAR_OWN, NEAR_SUM = (0, 1, 2, 3), (4, 6, 8, 10), (5, 7, 9, 11)
FAR2, OWN2, SUM2 = 12, 13, 14
SLOTS = 15


def block_at(axis, main, other):
    return other * SIDE + main if axis == 0 else main * SIDE + other


def kernel(
    n_section, n_shard,
    grads, params, m_first, m_second, layer, valid, decay,
    out_params, out_first, out_second, out_ratios,
    mine, theirs, landed, w_buf, f_buf, s_buf, upd, sums, got,
    load_sem, pair_send, pair_recv, link_send, link_recv, io_sem, out_sem, sum_send, sum_recv,
):
    rows = w_buf.shape[0]
    width = landed.shape[3]
    section, shard = lax.axis_index("section"), lax.axis_index("shard")
    core, x, y = shard % 2, (shard // 2) % SIDE, shard // (2 * SIDE)
    me = section * n_shard + shard
    partner = shard + 1 - 2 * core

    def shard_at(dy, dx):
        return (((y + dy) % SIDE) * SIDE + (x + dx) % SIDE) * 2 + core

    links = (shard_at(0, 1), shard_at(0, 3), shard_at(1, 0), shard_at(3, 0))

    barrier = pltpu.get_barrier_semaphore()
    for peer in (partner,) + links:
        pl.semaphore_signal(barrier, inc=1, device_id={"shard": peer}, device_id_type=MESH)
    for k in range(1, n_section):
        pl.semaphore_signal(
            barrier, inc=1, device_id={"section": (section + k) % n_section}, device_id_type=MESH
        )

    order = []
    for j in ORDER:
        order += [(h, block_at(h, 2, j)) for h in (0, 1)]
    for j in ORDER:
        for main in (1, 3, 0):
            order += [(h, block_at(h, main, j)) for h in (0, 1)]

    def rows_of(block, which):
        dy, dx = block // SIDE, block % SIDE
        chip = ((y + dy) % SIDE) * SIDE + (x + dx) % SIDE
        return pl.ds(pl.multiple_of(chip * (2 * rows) + which * rows, rows), rows)

    def load(h, block):
        return pltpu.make_async_copy(
            grads.at[0, 0, rows_of(block, core), pl.ds(h * 2 * width, 2 * width)],
            mine.at[h, block],
            load_sem.at[h, block],
        )

    def pair(h, block):
        return pltpu.make_async_remote_copy(
            src_ref=grads.at[0, 0, rows_of(block, 1 - core), pl.ds(h * 2 * width, 2 * width)],
            dst_ref=theirs.at[h, block],
            send_sem=pair_send.at[h, block],
            recv_sem=pair_recv.at[h, block],
            device_id={"shard": partner},
            device_id_type=MESH,
        )

    def quarter(ref, h, block, q):
        return ref.at[h, block, :, pl.ds(q * width, width)]

    def send(link, slot, src):
        return pltpu.make_async_remote_copy(
            src_ref=src,
            dst_ref=landed.at[link, slot],
            send_sem=link_send.at[link, slot],
            recv_sem=link_recv.at[link, slot],
            device_id={"shard": links[link]},
            device_id_type=MESH,
        )

    def arrived(link, slot):
        send(link, slot, landed.at[link, slot]).wait_recv()
        return landed.at[link, slot]

    def add_up(dst, terms):
        step = min(512, width)

        def one(i, _):
            cols = pl.ds(pl.multiple_of(i * step, step), step)
            total = terms[0][:, cols].astype(F32)
            for t in terms[1:]:
                total = total + t[:, cols].astype(F32)
            dst[:, cols] = total.astype(BF16)
            return 0

        lax.fori_loop(0, width // step, one, 0)

    for h, block in order:
        load(h, block).start()
    pl.semaphore_wait(barrier, 1 + len(links) + n_section - 1)
    for h, block in order:
        pair(h, block).start()
    io = [
        pltpu.make_async_copy(params.at[0], w_buf, io_sem.at[0]),
        pltpu.make_async_copy(m_first.at[0], f_buf, io_sem.at[1]),
        pltpu.make_async_copy(m_second.at[0], s_buf, io_sem.at[2]),
    ]
    for c in io:
        c.start()

    ready = set()

    def need(h, block):
        if (h, block) not in ready:
            ready.add((h, block))
            load(h, block).wait()
            pair(h, block).wait_recv()

    def put(link, slot, h, block, q, extra=()):
        need(h, block)
        dst = quarter(mine, h, block, q)
        add_up(dst, [dst, quarter(theirs, h, block, q), *extra])
        send(link, slot, dst).start()

    signs = (1, 3)

    def far(j):
        for axis in (0, 1):
            for d in (0, 1):
                put(2 * axis + d, FAR[j], axis, block_at(axis, 2, ORDER[j]), d)

    def near_own(j):
        for axis in (0, 1):
            for d in (0, 1):
                put(2 * axis + d, NEAR_OWN[j], axis, block_at(axis, signs[d], ORDER[j]), 1 - d)

    def near_sum(j):
        for axis in (0, 1):
            for d in (0, 1):
                link = 2 * axis + d
                put(link, NEAR_SUM[j], axis, block_at(axis, signs[d], ORDER[j]), d, [arrived(link, FAR[j])])

    def first_axis(axis, j):
        block = block_at(axis, 0, ORDER[j])
        need(axis, block)
        a, b = 2 * axis, 2 * axis + 1
        came = [arrived(link, slot) for link in (a, b) for slot in (NEAR_OWN[j], NEAR_SUM[j])]
        return block, ((came[1], came[2]), (came[3], came[0]))

    def settle(j):
        for axis in (0, 1):
            block, came = first_axis(axis, j)
            for q in (0, 1):
                dst = quarter(mine, axis, block, q)
                add_up(dst, [dst, quarter(theirs, axis, block, q), *came[q]])

    def far2():
        settle(0)
        for axis in (0, 1):
            for d in (0, 1):
                link = 2 * (1 - axis) + d
                send(link, FAR2, quarter(mine, axis, block_at(axis, 0, 2), d)).start()

    def own2():
        settle(1)
        settle(2)
        for axis in (0, 1):
            for d in (0, 1):
                link = 2 * (1 - axis) + d
                send(link, OWN2, quarter(mine, axis, block_at(axis, 0, signs[d]), 1 - d)).start()

    def sum2():
        for axis in (0, 1):
            for d in (0, 1):
                link = 2 * (1 - axis) + d
                dst = quarter(mine, axis, block_at(axis, 0, signs[d]), d)
                add_up(dst, [dst, arrived(link, FAR2)])
                send(link, SUM2, dst).start()

    for j in range(4):
        far(j)
    for j in range(3):
        near_own(j)
        near_sum(j)
    near_own(3)

    row_block = lax.broadcasted_iota(jnp.int32, (rows, 128), 0) // 8
    lane = lax.broadcasted_iota(jnp.int32, (1, 128), 1)
    blocks = rows // 8

    def per_row(values):
        out = jnp.full((rows, 128), values[0])
        for b in range(1, blocks):
            out = jnp.where(row_block == b, values[b], out)
        return out

    layers = [layer[0, b] for b in range(blocks)]
    lives = [valid[0, b] for b in range(blocks)]
    row_decay = per_row([decay[l] for l in layers])
    row_live = per_row(lives) > 0

    def by_layer(total, offset):
        out = jnp.zeros((1, 128), F32)
        for b in range(blocks):
            s = jnp.sum(total[8 * b : 8 * b + 8, :], keepdims=True)
            out = out + jnp.where((lane == layers[b] + offset) & (lives[b] > 0), s, 0.0)
        return out

    far2()
    near_sum(3)
    own2()
    sum2()

    for c in io:
        c.wait()
    columns = w_buf.shape[1]
    piece = 512

    def weights_sq(i, acc):
        for k in range(piece // 128):
            v = w_buf[:, pl.ds(pl.multiple_of(i * piece + k * 128, 128), 128)].astype(F32)
            acc = acc + v * v
        return acc

    w_sum = by_layer(lax.fori_loop(0, columns // piece, weights_sq, jnp.zeros((rows, 128), F32)), 8)

    acc = jnp.zeros((rows, 128), F32)
    for axis in (0, 1):
        block, came = first_axis(axis, 3)
        for q in (0, 1):
            a = 2 * (1 - axis)
            late = [arrived(a + q, SUM2), arrived(a + 1 - q, OWN2)]
            terms = [quarter(mine, axis, block, q), quarter(theirs, axis, block, q), *came[q], *late]
            base = (2 * axis + q) * width

            def one(i, acc, terms=terms, base=base):
                for k in range(min(512, width) // 128):
                    at = i * min(512, width) + k * 128
                    here = pl.ds(pl.multiple_of(at, 128), 128)
                    cols = pl.ds(pl.multiple_of(base + at, 128), 128)
                    g = terms[0][:, here].astype(F32)
                    for t in terms[1:]:
                        g = g + t[:, here].astype(F32)
                    old_f, old_s = f_buf[:, cols], s_buf[:, cols]
                    w = w_buf[:, cols].astype(F32)
                    first = 0.9 * old_f + 0.1 * g
                    second = 0.99 * old_s + 0.01 * g * g
                    u = (first * (1.0 / bias_first)) / (
                        jnp.sqrt(second * (1.0 / bias_second)) + 1e-06
                    ) + row_decay * w
                    upd[:, cols] = u
                    f_buf[:, cols] = jnp.where(row_live, first, old_f)
                    s_buf[:, cols] = jnp.where(row_live, second, old_s)
                    acc = acc + u * u
                return acc

            acc = lax.fori_loop(0, width // min(512, width), one, acc)

    vec = by_layer(acc, 0) + w_sum
    sums[0] = vec
    got[me] = vec

    n_all = n_section * n_shard

    def to_device(k):
        other = (me + k) % n_all
        return pltpu.make_async_remote_copy(
            src_ref=sums.at[0],
            dst_ref=got.at[me],
            send_sem=sum_send,
            recv_sem=sum_recv,
            device_id={"section": other // n_shard, "shard": other % n_shard},
            device_id_type=MESH,
        )

    def tell(k, _):
        to_device(k).start()
        return 0

    lax.fori_loop(1, n_all, tell, 0)
    outs = [
        pltpu.make_async_copy(f_buf, out_first.at[0], out_sem.at[0]),
        pltpu.make_async_copy(s_buf, out_second.at[0], out_sem.at[1]),
    ]
    for c in outs:
        c.start()
    everyone = pltpu.make_async_copy(got.at[pl.ds(0, n_all - 1)], got.at[pl.ds(0, n_all - 1)], sum_recv)
    everyone.wait()

    def add_device(k, t):
        return t + got[k]

    total = lax.fori_loop(0, n_all, add_device, jnp.zeros((1, 128), F32), unroll=8)
    wide = jnp.broadcast_to(total, (8, 128))
    ratios = jnp.sqrt(pltpu.roll(wide, 120, 1) / (wide + 1.0))[0:1]
    ratios = jnp.where(lane < 8, ratios, 0.0)
    out_ratios[...] = ratios
    scale = []
    for b in range(blocks):
        r = jnp.sum(jnp.where(lane == layers[b], ratios, 0.0), keepdims=True)
        scale.append(jnp.where(lives[b] > 0, 0.1 * r, 0.0))
    row_scale = per_row(scale)

    def last(i, _):
        for k in range(piece // 128):
            cols = pl.ds(pl.multiple_of(i * piece + k * 128, 128), 128)
            w = w_buf[:, cols].astype(F32)
            w_buf[:, cols] = (w - row_scale * upd[:, cols]).astype(BF16)
        return 0

    lax.fori_loop(0, columns // piece, last, 0)
    final = pltpu.make_async_copy(w_buf, out_params.at[0], out_sem.at[2])
    final.start()

    for h, block in order:
        pair(h, block).wait_send()
    for link in range(4):
        for slot in range(SLOTS):
            send(link, slot, landed.at[link, slot]).wait_send()
    pltpu.make_async_copy(got.at[pl.ds(0, n_all - 1)], got.at[pl.ds(0, n_all - 1)], sum_send).wait()
    for c in outs:
        c.wait()
    final.wait()


def shards(grad_parts, params, moment_first, moment_second, block_layer, block_valid, decay):
    rows, columns = params.shape[1:]
    n_section, n_shard = lax.axis_size("section"), lax.axis_size("shard")
    width = columns // 4
    chips = SIDE * SIDE
    anywhere, smem = pl.BlockSpec(memory_space=pl.ANY), pl.BlockSpec(memory_space=pltpu.SMEM)
    dma = pltpu.SemaphoreType.DMA
    new_params, new_first, new_second, ratios = pl.pallas_call(
        functools.partial(kernel, n_section, n_shard),
        out_shape=(
            jax.ShapeDtypeStruct(params.shape, params.dtype),
            jax.ShapeDtypeStruct(moment_first.shape, F32),
            jax.ShapeDtypeStruct(moment_second.shape, F32),
            jax.ShapeDtypeStruct((1, 128), F32),
        ),
        in_specs=[anywhere] * 4 + [smem] * 3,
        out_specs=(anywhere, anywhere, anywhere, pl.BlockSpec(memory_space=pltpu.VMEM)),
        scratch_shapes=[
            pltpu.VMEM((2, chips, rows, 2 * width), BF16),
            pltpu.VMEM((2, chips, rows, 2 * width), BF16),
            pltpu.VMEM((4, SLOTS, rows, width), BF16),
            pltpu.VMEM((rows, columns), BF16),
            pltpu.VMEM((rows, columns), F32),
            pltpu.VMEM((rows, columns), F32),
            pltpu.VMEM((rows, columns), F32),
            pltpu.VMEM((1, 1, 128), F32),
            pltpu.VMEM((n_section * n_shard, 1, 128), F32),
            dma((2, chips)),
            dma((2, chips)),
            dma((2, chips)),
            dma((4, SLOTS)),
            dma((4, SLOTS)),
            dma((3,)),
            dma((3,)),
            dma,
            dma,
        ],
        compiler_params=pltpu.CompilerParams(
            collective_id=0, has_side_effects=True, vmem_limit_bytes=56 * 2**20
        ),
        name="lamb_step",
    )(grad_parts, params, moment_first, moment_second, block_layer, block_valid, decay)
    return new_params, new_first, new_second, ratios[0, : decay.shape[0]]


def solution(mesh):
    placed = (
        P("section", "shard", None, None),
        P("section", "shard", None),
        P("section", "shard", None),
        P("section", "shard", None),
        P("section", "shard"),
        P("section", "shard"),
        P(),
    )
    return jax.shard_map(
        shards,
        mesh=mesh,
        in_specs=placed,
        out_specs=(
            P("section", "shard", None),
            P("section", "shard", None),
            P("section", "shard", None),
            P(),
        ),
        check_vma=False,
    )
```

time: 173 us -> 75.1 us (0.43); the launches traced: 170 us -> 74.8 us
  waiting for transfers between devices: 128 us -> 0 us
  Pallas kernels: 0 us -> 66.6 us
  between operations: 14.1 us -> 0.64 us
  blocking collectives: 13.1 us -> 0 us
  starting transfers between devices: 7.07 us -> 0 us
  local copies, waits for them, and re-layouts: 1.07 us -> 7.57 us
  other arithmetic: 5.5 us -> 0 us
    reduce_scatter x1 -> x0, waiting for transfers between devices: 121 us -> none  [shards(): lax.psum_scatter(local_grad.astype(jnp.float32).astype(jnp.bfloat16), 'sh...]
    pallas_call x0 -> x1, Pallas kernels: none -> 66.6 us  [shards(): pl.pallas_call(functools.partial(kernel, n_section, n_shard), out_shape=(...]
    all_gather x2 -> x0, blocking collectives: 13.1 us -> none  [the longest x1 7.89 us: carried_in(): gathered = lax.all_gather(part, axis)]
    all_to_all x1 -> x0, waiting for transfers between devices: 7.25 us -> none  [from_everyone(): lax.all_to_all(jnp.broadcast_to(x[None], (length, *x.shape)), axis, 0, 0,...]
    all_to_all x1 -> x0, starting transfers between devices: 7.04 us -> none  [from_everyone(): lax.all_to_all(jnp.broadcast_to(x[None], (length, *x.shape)), axis, 0, 0,...]
    unnamed x11 -> x3, local copies, waits for them, and re-layouts: 0.11 us -> 6.39 us
    reduce_sum x2 -> x0, other arithmetic: 3.85 us -> none  [the longest x1 3.8 us: shards(): jnp.sum(update * update, axis=-1)]
  transfers between devices with their start and end apart: 2 -> 0, of which waited for: 2 -> 0; matrix products, arithmetic and copies ran while one was open for 0% -> 0% of each run, Pallas kernels for 0% -> 0%
where the time goes in v1:
time: 75.1 us; the launch traced here: 74.8 us
  Pallas kernels  66.6 us (89%)
  local copies, waits for them, and re-layouts  7.57 us (10%)
    pallas_call x1, Pallas kernels, shards(): pl.pallas_call(functools.partial(kernel, n_section, n_shard), out_shape=(...  66.6 us
    unnamed x3, local copies, waits for them, and re-layouts  6.39 us

profile of v1, /device:TPU:1, one launch (start us, length us, event | category | flops | bytes accessed | tf_op | source)
XLA Modules:
  0.0 74.8 jit_solution(14954247852287293710)
XLA Ops:
  0.6 66.6 %lamb_step.1 = (bf16[1,32,8192]{2,1,0:T(8,128)(2,1)}, f32[1,32,8192]{2,1,0:T(8,128)}, f32[1,32,8192]{2,1,0:T(8,128)}, f32[1,128]{1,0:T(1,128)}) custom-call(bf16[1,1,1024,8192]{3,2,1,0:T(8,128)(2,1)} %grads.1, bf16[1,32,8192]{2,1,0:T(8,128)(2,1)} %params.1, f32[1,32,8192]{2,1,0:T(8,128)} %m_first.1, f32[1,32,8192]{2,1,0:T(8,128)} %m_second.1, s32[1,4]{1,0:T(1,128)} %layer.1, ...), custom_call_target="tpu_custom_call" | custom-call | tf_op jit(solution)/shard_map/lamb_step/pallas_call | solution.py:347
  67.3 1.2 %slice_bitcast_fusion = f32[8]{0:T(128)} fusion(f32[1,128]{1,0:T(1,128)} %get-tuple-element.11), kind=kLoop, calls=%fused_computation | loop fusion | bytes 64 | tf_op jit(solution)/shard_map/squeeze | solution.py:382
  68.4 1.9 %copy.14 = bf16[1,32,8192]{2,1,0:T(8,128)(2,1)} copy(bf16[1,32,8192]{2,1,0:T(8,128)(2,1)} %get-tuple-element.16) | data formatting | bytes 1048576
  70.3 2.3 %copy.15 = f32[1,32,8192]{2,1,0:T(8,128)} copy(f32[1,32,8192]{2,1,0:T(8,128)} %get-tuple-element.17) | data formatting | bytes 2097152
  72.6 2.3 %copy.16 = f32[1,32,8192]{2,1,0:T(8,128)} copy(f32[1,32,8192]{2,1,0:T(8,128)} %get-tuple-element.18) | data formatting | bytes 2097152

commit v2 on v0

v2 whole, which is shorter than its diff:
```python
import functools

import jax
import jax.numpy as jnp
from jax import lax
from jax.experimental import pallas as pl
from jax.experimental.pallas import tpu as pltpu
from jax.sharding import PartitionSpec as P

bias_first = 1.0 - 0.9**10
bias_second = 1.0 - 0.99**10

MESH = pl.DeviceIdType.MESH
F32, BF16 = jnp.float32, jnp.bfloat16
SIDE = 4
ORDER = (2, 1, 3, 0)
FAR, NEAR_OWN, NEAR_SUM = (0, 1, 2, 3), (4, 6, 8, 10), (5, 7, 9, 11)
FAR2, OWN2 = 12, 13
SLOTS = 14


def block_at(axis, main, other):
    return other * SIDE + main if axis == 0 else main * SIDE + other


def kernel(
    n_section, n_shard,
    grads, params, m_first, m_second, layer_hbm, valid_hbm, decay_hbm,
    upd, f_buf, s_buf, w_buf, out_scale, out_ratios,
    mine, theirs, ahead, landed, late, layer, valid, decay, sums, got,
    load_sem, pair_send, pair_recv, link_send, far_recv, near_recv, far2_recv, own2_recv, sum2_recv, sum2_send,
    io_sem, sum_send, sum_recv,
):
    rows = w_buf.shape[1]
    columns = w_buf.shape[2]
    width = landed.shape[3]
    part = late.shape[3]
    parts = width // part
    section, shard = lax.axis_index("section"), lax.axis_index("shard")
    core, x, y = lax.rem(shard, 2), lax.rem(lax.div(shard, 2), SIDE), lax.div(shard, 2 * SIDE)
    me = section * n_shard + shard
    partner = shard + 1 - 2 * core

    def chip_at(dy, dx):
        return lax.rem(y + dy, SIDE) * SIDE + lax.rem(x + dx, SIDE)

    links = tuple(chip_at(dy, dx) * 2 + core for dy, dx in ((0, 1), (0, 3), (1, 0), (3, 0)))

    barrier = pltpu.get_barrier_semaphore()
    for peer in (partner,) + links:
        pl.semaphore_signal(barrier, inc=1, device_id={"shard": peer}, device_id_type=MESH)
    for k in range(1, n_section):
        pl.semaphore_signal(
            barrier, inc=1, device_id={"section": lax.rem(section + k, n_section)}, device_id_type=MESH
        )

    groups = [[(0, block_at(0, 2, 2))], [(1, block_at(1, 2, 2))]]
    for j in ORDER[1:]:
        groups.append([(h, block_at(h, 2, j)) for h in (0, 1)])
    for j in ORDER:
        groups.append([(h, block_at(h, main, j)) for main in (1, 3, 0) for h in (0, 1)])
    group_of = {b: g for g, blocks in enumerate(groups) for b in blocks}

    def source(h, block, which):
        chip = chip_at(block // SIDE, block % SIDE)
        at = pl.multiple_of(chip * (2 * rows) + which * rows, rows)
        return grads.at[0, 0, pl.ds(at, rows), pl.ds(h * 2 * width, 2 * width)]

    def load(h, block):
        return pltpu.make_async_copy(
            source(h, block, core), mine.at[h, block], load_sem.at[group_of[h, block]]
        )

    def fetch_ahead(h):
        return pltpu.make_async_copy(source(h, block_at(h, 2, 2), 1 - core), ahead.at[h], io_sem.at[h])

    def pair(h, block):
        first = group_of[h, block] < 2
        return pltpu.make_async_remote_copy(
            src_ref=ahead.at[h] if first else source(h, block, 1 - core),
            dst_ref=theirs.at[h, block],
            send_sem=pair_send,
            recv_sem=pair_recv.at[group_of[h, block]],
            device_id={"shard": partner},
            device_id_type=MESH,
        )

    def wait_bytes(ref, sem):
        pltpu.make_async_copy(ref, ref, sem).wait()

    def quarter(ref, h, block, q):
        return ref.at[h, block, :, pl.ds(q * width, width)]

    def send(link, src, dst, recv_sem, send_sem=link_send):
        pltpu.make_async_remote_copy(
            src_ref=src,
            dst_ref=dst,
            send_sem=send_sem,
            recv_sem=recv_sem,
            device_id={"shard": links[link]},
            device_id_type=MESH,
        ).start()

    def add_up(dst, terms):
        size = dst.shape[1]
        step = min(512, size)

        def one(i, _):
            cols = pl.ds(pl.multiple_of(i * step, step), step)
            if len(terms) == 2:
                dst[:, cols] = terms[0][:, cols] + terms[1][:, cols]
            else:
                total = terms[0][:, cols].astype(F32)
                for t in terms[1:]:
                    total = total + t[:, cols].astype(F32)
                dst[:, cols] = total.astype(BF16)
            return 0

        lax.fori_loop(0, size // step, one, 0)

    for h in (0, 1):
        fetch_ahead(h).start()
        load(h, block_at(h, 2, 2)).start()
    for h, block in groups[2]:
        load(h, block).start()
    with jax.named_scope("barrier"):
        pl.semaphore_wait(barrier, 1 + len(links) + n_section - 1)
    for h in (0, 1):
        fetch_ahead(h).wait()
        pair(h, block_at(h, 2, 2)).start()
    small = [
        pltpu.make_async_copy(a, b, io_sem.at[2 + k])
        for k, (a, b) in enumerate(((layer_hbm, layer), (valid_hbm, valid), (decay_hbm, decay)))
    ]
    io = [
        pltpu.make_async_copy(params, w_buf, io_sem.at[5]),
        pltpu.make_async_copy(m_first, f_buf, io_sem.at[6]),
        pltpu.make_async_copy(m_second, s_buf, io_sem.at[7]),
    ]
    for g in range(2, len(groups)):
        for h, block in groups[g]:
            pair(h, block).start()
        if g > 2:
            for h, block in groups[g]:
                load(h, block).start()
        if g == 5:
            for c in small + io:
                c.start()

    ready = set()

    def need(h, block):
        g = group_of[h, block]
        if g not in ready:
            ready.add(g)
            several = mine.at[0, pl.ds(0, len(groups[g]))]
            wait_bytes(several, load_sem.at[g])
            wait_bytes(several, pair_recv.at[g])

    signs = (1, 3)
    each = [(axis, d, 2 * axis + d) for axis in (0, 1) for d in (0, 1)]
    four = landed.at[0, pl.ds(0, 4)]

    def own_terms(axis, block, q):
        need(axis, block)
        return [quarter(mine, axis, block, q), quarter(theirs, axis, block, q)]

    def far(j):
        for axis, d, link in each:
            terms = own_terms(axis, block_at(axis, 2, ORDER[j]), d)
            add_up(terms[0], terms)
            send(link, terms[0], landed.at[link, FAR[j]], far_recv.at[j])

    def near_own(j):
        for axis, d, link in each:
            terms = own_terms(axis, block_at(axis, signs[d], ORDER[j]), 1 - d)
            add_up(terms[0], terms)
            send(link, terms[0], landed.at[link, NEAR_OWN[j]], near_recv.at[axis, j])

    def near_sum(j):
        wait_bytes(four, far_recv.at[j])
        for axis, d, link in each:
            terms = own_terms(axis, block_at(axis, signs[d], ORDER[j]), d)
            add_up(terms[0], terms + [landed.at[link, FAR[j]]])
            send(link, terms[0], landed.at[link, NEAR_SUM[j]], near_recv.at[axis, j])

    def first_axis(axis, j):
        block = block_at(axis, 0, ORDER[j])
        wait_bytes(four, near_recv.at[axis, j])
        a, b = 2 * axis, 2 * axis + 1
        return [
            own_terms(axis, block, q)
            + [landed.at[(a, b)[q], NEAR_SUM[j]], landed.at[(b, a)[q], NEAR_OWN[j]]]
            for q in (0, 1)
        ]

    def settle(j):
        for axis in (0, 1):
            for terms in first_axis(axis, j):
                add_up(terms[0], terms)

    def far2():
        settle(0)
        for axis, d, _ in each:
            link = 2 * (1 - axis) + d
            send(link, quarter(mine, axis, block_at(axis, 0, 2), d), landed.at[link, FAR2], far2_recv)

    def own2():
        settle(1)
        settle(2)
        for axis, d, _ in each:
            link = 2 * (1 - axis) + d
            src = quarter(mine, axis, block_at(axis, 0, signs[d]), 1 - d)
            send(link, src, landed.at[link, OWN2], own2_recv)

    def sum2():
        wait_bytes(four, far2_recv)
        for p in range(parts):
            for axis, d, _ in each:
                link = 2 * (1 - axis) + d
                at = pl.ds(p * part, part)
                dst = quarter(mine, axis, block_at(axis, 0, signs[d]), d).at[:, at]
                add_up(dst, [dst, landed.at[link, FAR2].at[:, at]])
                send(link, dst, late.at[p, link], sum2_recv.at[p], sum2_send)

    for j in range(4):
        with jax.named_scope(f"far{j}"):
            far(j)
    for j in range(3):
        with jax.named_scope(f"own{j}"):
            near_own(j)
        with jax.named_scope(f"sum{j}"):
            near_sum(j)
    near_own(3)

    for c in small + io:
        c.wait()
    row_block = lax.broadcasted_iota(jnp.int32, (rows, 128), 0) // 8
    lane = lax.broadcasted_iota(jnp.int32, (1, 128), 1)
    blocks = rows // 8

    def per_row(values):
        out = jnp.full((rows, 128), values[0])
        for b in range(1, blocks):
            out = jnp.where(row_block == b, values[b], out)
        return out

    layers = [layer[0, b] for b in range(blocks)]
    lives = [valid[0, b] for b in range(blocks)]
    row_decay = per_row([decay[l] for l in layers])
    row_live = per_row(lives) > 0

    def by_layer(total, offset):
        out = jnp.zeros((1, 128), F32)
        for b in range(blocks):
            s = jnp.sum(total[8 * b : 8 * b + 8, :], keepdims=True)
            out = out + jnp.where((lane == layers[b] + offset) & (lives[b] > 0), s, 0.0)
        return out

    piece = 512

    def weights_sq(i, acc):
        for k in range(piece // 128):
            v = w_buf[0, :, pl.ds(pl.multiple_of(i * piece + k * 128, 128), 128)].astype(F32)
            acc = acc + v * v
        return acc

    w_sum = by_layer(lax.fori_loop(0, columns // piece, weights_sq, jnp.zeros((rows, 128), F32)), 8)

    with jax.named_scope("far2"):
        far2()
    with jax.named_scope("near_sum3"):
        near_sum(3)
    with jax.named_scope("own2"):
        own2()
    with jax.named_scope("sum2"):
        sum2()

    with jax.named_scope("early"):
        for axis in (0, 1):
            both = first_axis(axis, 3)
            if axis == 0:
                wait_bytes(four, own2_recv)
            for q in (0, 1):
                terms = both[q] + [landed.at[2 * (1 - axis) + 1 - q, OWN2]]
                base = (2 * axis + q) * width

                def before(i, _, terms=terms, base=base):
                    at = pl.multiple_of(i * min(512, width), min(512, width))
                    here = pl.ds(at, min(512, width))
                    g = terms[0][:, here].astype(F32)
                    for t in terms[1:]:
                        g = g + t[:, here].astype(F32)
                    upd[0, :, pl.ds(base + at, min(512, width))] = g
                    return 0

                lax.fori_loop(0, width // min(512, width), before, 0)

    acc = jnp.zeros((rows, 128), F32)
    for p in range(parts):
        with jax.named_scope(f"late{p}"):
            wait_bytes(late.at[p], sum2_recv.at[p])
        for axis in (0, 1):
            for q in (0, 1):
                came = late.at[p, 2 * (1 - axis) + q]
                base = (2 * axis + q) * width + p * part
                step = min(512, part)

                def one(i, acc, came=came, base=base, step=step):
                    for k in range(step // 128):
                        at = i * step + k * 128
                        cols = pl.ds(pl.multiple_of(base + at, 128), 128)
                        g = upd[0, :, cols] + came[:, pl.ds(pl.multiple_of(at, 128), 128)].astype(F32)
                        old_f, old_s = f_buf[0, :, cols], s_buf[0, :, cols]
                        w = w_buf[0, :, cols].astype(F32)
                        first = 0.9 * old_f + 0.1 * g
                        second = 0.99 * old_s + 0.01 * g * g
                        u = (first * (1.0 / bias_first)) / (
                            jnp.sqrt(second * (1.0 / bias_second)) + 1e-06
                        ) + row_decay * w
                        upd[0, :, cols] = u
                        f_buf[0, :, cols] = jnp.where(row_live, first, old_f)
                        s_buf[0, :, cols] = jnp.where(row_live, second, old_s)
                        acc = acc + u * u
                    return acc

                acc = lax.fori_loop(0, part // step, one, acc)

    vec = by_layer(acc, 0) + w_sum
    sums[0] = vec
    got[me] = vec

    def tell(to_section, to_shard):
        pltpu.make_async_remote_copy(
            src_ref=sums.at[0],
            dst_ref=got.at[me],
            send_sem=sum_send,
            recv_sem=sum_recv,
            device_id={"section": to_section, "shard": to_shard},
            device_id_type=MESH,
        ).start()

    sections = [lax.rem(section + k, n_section) for k in range(n_section)]

    def tell_shard(k, _):
        to_shard = lax.rem(shard + k, n_shard)
        for to_section in sections:
            tell(to_section, to_shard)
        return 0

    with jax.named_scope("tell"):
        lax.fori_loop(1, n_shard, tell_shard, 0)
        for to_section in sections[1:]:
            tell(to_section, shard)
    n_all = n_section * n_shard
    others = got.at[pl.ds(0, n_all - 1)]
    with jax.named_scope("everyone"):
        wait_bytes(others, sum_recv)

    def add_device(k, t):
        return t + got[k]

    total = lax.fori_loop(0, n_all, add_device, jnp.zeros((1, 128), F32), unroll=8)
    wide = jnp.broadcast_to(total, (8, 128))
    ratios = jnp.sqrt(pltpu.roll(wide, 120, 1) / (wide + 1.0))[0:1]
    ratios = jnp.where(lane < 8, ratios, 0.0)
    out_ratios[...] = ratios
    scale = []
    for b in range(blocks):
        r = jnp.sum(jnp.where(lane == layers[b], ratios, 0.0), keepdims=True)
        scale.append(jnp.where(lives[b] > 0, 0.1 * r, 0.0))
    out_scale[...] = per_row(scale)

    with jax.named_scope("drain"):
        wait_bytes(theirs, pair_send)
        wait_bytes(landed, link_send)
        wait_bytes(late, sum2_send)
        wait_bytes(others, sum_send)


def finish(upd, first, second, weights, scale, ratios, out_params, out_first, out_second, out_ratios, stage, sem):
    columns = stage.shape[1]
    step = columns // 4
    copies = [
        pltpu.make_async_copy(first, out_first, sem.at[0]),
        pltpu.make_async_copy(second, out_second, sem.at[1]),
    ]
    for c in copies:
        c.start()
    out_ratios[...] = ratios[:, : out_ratios.shape[1]]
    row_scale = scale[...]
    for n in range(4):

        def one(i, _, n=n):
            for k in range(4):
                cols = pl.ds(pl.multiple_of(n * step + i * 512 + k * 128, 128), 128)
                w = weights[0, :, cols].astype(F32)
                stage[:, cols] = (w - row_scale * upd[0, :, cols]).astype(BF16)
            return 0

        lax.fori_loop(0, step // 512, one, 0)
        cols = pl.ds(n * step, step)
        c = pltpu.make_async_copy(stage.at[:, cols], out_params.at[0, :, cols], sem.at[2 + n])
        c.start()
        copies.append(c)
    for c in copies:
        c.wait()


PARTS = 4


def shards(grad_parts, params, moment_first, moment_second, block_layer, block_valid, decay):
    rows, columns = params.shape[1:]
    n_section, n_shard = lax.axis_size("section"), lax.axis_size("shard")
    width = columns // 4
    chips = SIDE * SIDE
    hbm, vmem = pl.BlockSpec(memory_space=pltpu.HBM), pl.BlockSpec(memory_space=pltpu.VMEM)
    dma = pltpu.SemaphoreType.DMA
    groups = 9
    upd, first, second, weights, scale, ratios = pl.pallas_call(
        functools.partial(kernel, n_section, n_shard),
        out_shape=(
            pltpu.VMEM(moment_first.shape, F32),
            pltpu.VMEM(moment_first.shape, F32),
            pltpu.VMEM(moment_first.shape, F32),
            pltpu.VMEM(params.shape, BF16),
            pltpu.VMEM((rows, 128), F32),
            pltpu.VMEM((1, 128), F32),
        ),
        in_specs=[hbm] * 7,
        out_specs=(vmem,) * 6,
        scratch_shapes=[
            pltpu.VMEM((2, chips, rows, 2 * width), BF16),
            pltpu.VMEM((2, chips, rows, 2 * width), BF16),
            pltpu.VMEM((2, rows, 2 * width), BF16),
            pltpu.VMEM((4, SLOTS, rows, width), BF16),
            pltpu.VMEM((PARTS, 4, rows, width // PARTS), BF16),
            pltpu.SMEM(block_layer.shape, jnp.int32),
            pltpu.SMEM(block_valid.shape, jnp.int32),
            pltpu.SMEM(decay.shape, F32),
            pltpu.VMEM((1, 1, 128), F32),
            pltpu.VMEM((n_section * n_shard, 1, 128), F32),
            dma((groups,)),
            dma,
            dma((groups,)),
            dma,
            dma((4,)),
            dma((2, 4)),
            dma,
            dma,
            dma((PARTS,)),
            dma,
            dma((8,)),
            dma,
            dma,
        ],
        compiler_params=pltpu.CompilerParams(
            collective_id=0, has_side_effects=True, vmem_limit_bytes=48 * 2**20
        ),
        name="lamb_step",
    )(*(
        pltpu.with_memory_space_constraint(a, pltpu.HBM)
        for a in (grad_parts, params, moment_first, moment_second, block_layer, block_valid, decay)
    ))
    new_params, new_first, new_second, ratios = pl.pallas_call(
        finish,
        out_shape=(
            jax.ShapeDtypeStruct(params.shape, params.dtype),
            jax.ShapeDtypeStruct(moment_first.shape, F32),
            jax.ShapeDtypeStruct(moment_second.shape, F32),
            jax.ShapeDtypeStruct((1, decay.shape[0]), F32),
        ),
        in_specs=[vmem] * 6,
        out_specs=(hbm, hbm, hbm, vmem),
        scratch_shapes=[pltpu.VMEM((rows, columns), BF16), dma((6,))],
        compiler_params=pltpu.CompilerParams(vmem_limit_bytes=8 * 2**20),
        name="finish",
    )(upd, first, second, weights, scale, ratios)
    return new_params, new_first, new_second, ratios[0]


def solution(mesh):
    placed = (
        P("section", "shard", None, None),
        P("section", "shard", None),
        P("section", "shard", None),
        P("section", "shard", None),
        P("section", "shard"),
        P("section", "shard"),
        P(),
    )
    return jax.shard_map(
        shards,
        mesh=mesh,
        in_specs=placed,
        out_specs=(
            P("section", "shard", None),
            P("section", "shard", None),
            P("section", "shard", None),
            P(),
        ),
        check_vma=False,
    )
```

time: 173 us -> 63.2 us (0.37); the launches traced: 170 us -> 63 us
  waiting for transfers between devices: 128 us -> 0 us
  Pallas kernels: 0 us -> 62.4 us
  between operations: 14.1 us -> 0.64 us
  blocking collectives: 13.1 us -> 0 us
  starting transfers between devices: 7.07 us -> 0 us
  other arithmetic: 5.5 us -> 0 us
    reduce_scatter x1 -> x0, waiting for transfers between devices: 121 us -> none  [shards(): lax.psum_scatter(local_grad.astype(jnp.float32).astype(jnp.bfloat16), 'sh...]
    pallas_call x0 -> x2, Pallas kernels: none -> 62.4 us  [the longest x1 60.4 us: shards(): pl.pallas_call(functools.partial(kernel, n_section, n_shard), out_shape=(...]
    all_gather x2 -> x0, blocking collectives: 13.1 us -> none  [the longest x1 7.89 us: carried_in(): gathered = lax.all_gather(part, axis)]
    all_to_all x1 -> x0, waiting for transfers between devices: 7.25 us -> none  [from_everyone(): lax.all_to_all(jnp.broadcast_to(x[None], (length, *x.shape)), axis, 0, 0,...]
    all_to_all x1 -> x0, starting transfers between devices: 7.04 us -> none  [from_everyone(): lax.all_to_all(jnp.broadcast_to(x[None], (length, *x.shape)), axis, 0, 0,...]
    reduce_sum x2 -> x0, other arithmetic: 3.85 us -> none  [the longest x1 3.8 us: shards(): jnp.sum(update * update, axis=-1)]
  transfers between devices with their start and end apart: 2 -> 0, of which waited for: 2 -> 0; matrix products, arithmetic and copies ran while one was open for 0% -> 0% of each run, Pallas kernels for 0% -> 0%
where the time goes in v2:
time: 63.2 us; the launch traced here: 63 us
  Pallas kernels  62.4 us (99%)
  between operations  0.64 us (1%)
    pallas_call x1, Pallas kernels, shards(): pl.pallas_call(functools.partial(kernel, n_section, n_shard), out_shape=(...  60.4 us
    pallas_call x1, Pallas kernels, shards(): pl.pallas_call(finish, out_shape=(jax.ShapeDtypeStruct(params.shape, para...  2.04 us

profile of v2, /device:TPU:1, one launch (start us, length us, event | category | flops | bytes accessed | tf_op | source)
XLA Modules:
  0.0 63.0 jit_solution(11193788160411147004)
XLA Ops:
  0.6 60.4 %lamb_step.1 = (f32[1,32,8192]{2,1,0:T(8,128)S(1)}, f32[1,32,8192]{2,1,0:T(8,128)S(1)}, f32[1,32,8192]{2,1,0:T(8,128)S(1)}, bf16[1,32,8192]{2,1,0:T(8,128)(2,1)S...) custom-call(bf16[1,1,1024,8192]{3,2,1,0:T(8,128)(2,1)} %grads.1, bf16[1,32,8192]{2,1,0:T(8,128)(2,1)} %params.1, ...), custom_call_target="tpu_custom_call" | custom-call | tf_op jit(solution)/shard_map/lamb_step/pallas_call | solution.py:421
  61.0 2.0 %finish.1 = (bf16[1,32,8192]{2,1,0:T(8,128)(2,1)}, f32[1,32,8192]{2,1,0:T(8,128)}, f32[1,32,8192]{2,1,0:T(8,128)}, f32[1,8]{1,0:T(1,128)}) custom-call(f32[1,32,8192]{2,1,0:T(8,128)S(1)} %get-tuple-element.14.upd, f32[1,32,8192]{2,1,0:T(8,128)S(1)} %get-tuple-element.15.first, f32[1,32,8192]{2,1,0:T(8,128)S(1)} %get-tuple-element.16.second, ...), custom_call_target="tpu_custom_call" | custom-call | tf_op jit(solution)/shard_map/finish/pallas_call | solution.py:466

commit v3 on v2

--- a/solution.py
+++ b/solution.py
@@ -28,8 +28,8 @@
     grads, params, m_first, m_second, layer_hbm, valid_hbm, decay_hbm,
     upd, f_buf, s_buf, w_buf, out_scale, out_ratios,
     mine, theirs, ahead, landed, late, layer, valid, decay, sums, got,
-    load_sem, pair_send, pair_recv, link_send, far_recv, near_recv, far2_recv, own2_recv, sum2_recv, sum2_send,
-    io_sem, sum_send, sum_recv,
+    here_sem, pair_send, link_send, far_recv, near_recv, far2_recv, own2_recv, sum2_recv, sum2_send,
+    start_recv, ahead_sem, small_sem, io_sem, sum_send, sum_recv,
 ):
     rows = w_buf.shape[1]
     columns = w_buf.shape[2]
@@ -54,8 +54,8 @@
             barrier, inc=1, device_id={"section": lax.rem(section + k, n_section)}, device_id_type=MESH
         )
 
-    groups = [[(0, block_at(0, 2, 2))], [(1, block_at(1, 2, 2))]]
-    for j in ORDER[1:]:
+    groups = []
+    for j in ORDER:
         groups.append([(h, block_at(h, 2, j)) for h in (0, 1)])
     for j in ORDER:
         groups.append([(h, block_at(h, main, j)) for main in (1, 3, 0) for h in (0, 1)])
@@ -68,19 +68,31 @@
 
     def load(h, block):
         return pltpu.make_async_copy(
-            source(h, block, core), mine.at[h, block], load_sem.at[group_of[h, block]]
+            source(h, block, core), mine.at[h, block], here_sem.at[group_of[h, block]]
         )
 
     def fetch_ahead(h):
-        return pltpu.make_async_copy(source(h, block_at(h, 2, 2), 1 - core), ahead.at[h], io_sem.at[h])
+        return pltpu.make_async_copy(source(h, block_at(h, 2, 2), 1 - core), ahead.at[h], ahead_sem)
 
     def pair(h, block):
-        first = group_of[h, block] < 2
         return pltpu.make_async_remote_copy(
-            src_ref=ahead.at[h] if first else source(h, block, 1 - core),
+            src_ref=source(h, block, 1 - core),
             dst_ref=theirs.at[h, block],
             send_sem=pair_send,
-            recv_sem=pair_recv.at[group_of[h, block]],
+            recv_sem=here_sem.at[group_of[h, block]],
+            device_id={"shard": partner},
+            device_id_type=MESH,
+        )
+
+    size0 = width // PARTS0
+
+    def pair0(p, h, q):
+        cols = pl.ds(q * width + p * size0, size0)
+        return pltpu.make_async_remote_copy(
+            src_ref=ahead.at[h, :, cols],
+            dst_ref=theirs.at[h, block_at(h, 2, 2), :, cols],
+            send_sem=pair_send,
+            recv_sem=start_recv.at[p],
             device_id={"shard": partner},
             device_id_type=MESH,
         )
@@ -121,49 +133,59 @@
     for h in (0, 1):
         fetch_ahead(h).start()
         load(h, block_at(h, 2, 2)).start()
-    for h, block in groups[2]:
+    for h, block in groups[1]:
         load(h, block).start()
     with jax.named_scope("barrier"):
         pl.semaphore_wait(barrier, 1 + len(links) + n_section - 1)
-    for h in (0, 1):
-        fetch_ahead(h).wait()
-        pair(h, block_at(h, 2, 2)).start()
+    wait_bytes(ahead, ahead_sem)
+    for p in range(PARTS0):
+        for h in (0, 1):
+            for q in (0, 1):
+                pair0(p, h, q).start()
     small = [
-        pltpu.make_async_copy(a, b, io_sem.at[2 + k])
+        pltpu.make_async_copy(a, b, small_sem.at[k])
         for k, (a, b) in enumerate(((layer_hbm, layer), (valid_hbm, valid), (decay_hbm, decay)))
     ]
     io = [
-        pltpu.make_async_copy(params, w_buf, io_sem.at[5]),
-        pltpu.make_async_copy(m_first, f_buf, io_sem.at[6]),
-        pltpu.make_async_copy(m_second, s_buf, io_sem.at[7]),
+        pltpu.make_async_copy(params, w_buf, io_sem.at[0]),
+        pltpu.make_async_copy(m_first, f_buf, io_sem.at[1]),
+        pltpu.make_async_copy(m_second, s_buf, io_sem.at[1]),
     ]
-    for g in range(2, len(groups)):
+    for g in range(1, len(groups)):
         for h, block in groups[g]:
             pair(h, block).start()
-        if g > 2:
+        if g > 1:
             for h, block in groups[g]:
                 load(h, block).start()
-        if g == 5:
+        if g == 4:
             for c in small + io:
                 c.start()
 
-    ready = set()
+    ready = {0}
 
     def need(h, block):
         g = group_of[h, block]
         if g not in ready:
             ready.add(g)
-            several = mine.at[0, pl.ds(0, len(groups[g]))]
-            wait_bytes(several, load_sem.at[g])
-            wait_bytes(several, pair_recv.at[g])
+            wait_bytes(mine.at[0, pl.ds(0, 2 * len(groups[g]))], here_sem.at[g])
 
     signs = (1, 3)
     each = [(axis, d, 2 * axis + d) for axis in (0, 1) for d in (0, 1)]
-    four = landed.at[0, pl.ds(0, 4)]
+    four, eight = landed.at[0, pl.ds(0, 4)], landed.at[0, pl.ds(0, 8)]
 
     def own_terms(axis, block, q):
         need(axis, block)
         return [quarter(mine, axis, block, q), quarter(theirs, axis, block, q)]
+
+    def far_first():
+        wait_bytes(mine.at[0, pl.ds(0, 2)], here_sem.at[0])
+        for p in range(PARTS0):
+            wait_bytes(late.at[pl.ds(0, PARTS // PARTS0)], start_recv.at[p])
+            for axis, d, link in each:
+                here = pl.ds(p * size0, size0)
+                terms = [t.at[:, here] for t in own_terms(axis, block_at(axis, 2, 2), d)]
+                add_up(terms[0], terms)
+                send(link, terms[0], landed.at[link, FAR[0], :, here], far_recv.at[0])
 
     def far(j):
         for axis, d, link in each:
@@ -175,18 +197,17 @@
         for axis, d, link in each:
             terms = own_terms(axis, block_at(axis, signs[d], ORDER[j]), 1 - d)
             add_up(terms[0], terms)
-            send(link, terms[0], landed.at[link, NEAR_OWN[j]], near_recv.at[axis, j])
+            send(link, terms[0], landed.at[link, NEAR_OWN[j]], near_recv.at[j])
 
     def near_sum(j):
         wait_bytes(four, far_recv.at[j])
         for axis, d, link in each:
             terms = own_terms(axis, block_at(axis, signs[d], ORDER[j]), d)
             add_up(terms[0], terms + [landed.at[link, FAR[j]]])
-            send(link, terms[0], landed.at[link, NEAR_SUM[j]], near_recv.at[axis, j])
+            send(link, terms[0], landed.at[link, NEAR_SUM[j]], near_recv.at[j])
 
     def first_axis(axis, j):
         block = block_at(axis, 0, ORDER[j])
-        wait_bytes(four, near_recv.at[axis, j])
         a, b = 2 * axis, 2 * axis + 1
         return [
             own_terms(axis, block, q)
@@ -195,6 +216,7 @@
         ]
 
     def settle(j):
+        wait_bytes(eight, near_recv.at[j])
         for axis in (0, 1):
             for terms in first_axis(axis, j):
                 add_up(terms[0], terms)
@@ -223,7 +245,9 @@
                 add_up(dst, [dst, landed.at[link, FAR2].at[:, at]])
                 send(link, dst, late.at[p, link], sum2_recv.at[p], sum2_send)
 
-    for j in range(4):
+    with jax.named_scope("far0"):
+        far_first()
+    for j in range(1, 4):
         with jax.named_scope(f"far{j}"):
             far(j)
     for j in range(3):
@@ -233,8 +257,9 @@
             near_sum(j)
     near_own(3)
 
-    for c in small + io:
+    for c in small + io[:1]:
         c.wait()
+    wait_bytes(theirs.at[0, pl.ds(0, 8)], io_sem.at[1])
     row_block = lax.broadcasted_iota(jnp.int32, (rows, 128), 0) // 8
     lane = lax.broadcasted_iota(jnp.int32, (1, 128), 1)
     blocks = rows // 8
@@ -250,12 +275,14 @@
     row_decay = per_row([decay[l] for l in layers])
     row_live = per_row(lives) > 0
 
-    def by_layer(total, offset):
-        out = jnp.zeros((1, 128), F32)
-        for b in range(blocks):
-            s = jnp.sum(total[8 * b : 8 * b + 8, :], keepdims=True)
-            out = out + jnp.where((lane == layers[b] + offset) & (lives[b] > 0), s, 0.0)
-        return out
+    row_layer = per_row(layers)
+    row_lane = lax.broadcasted_iota(jnp.int32, (rows, 128), 1)
+    own_lane = (row_lane == row_layer) & row_live
+    own_lane_w = (row_lane == row_layer + 8) & row_live
+
+    def by_layer(total, lanes):
+        in_row = jnp.sum(total, axis=1, keepdims=True)
+        return jnp.sum(jnp.where(lanes, in_row, 0.0), axis=0, keepdims=True)
 
     piece = 512
 
@@ -265,7 +292,7 @@
             acc = acc + v * v
         return acc
 
-    w_sum = by_layer(lax.fori_loop(0, columns // piece, weights_sq, jnp.zeros((rows, 128), F32)), 8)
+    w_sum = by_layer(lax.fori_loop(0, columns // piece, weights_sq, jnp.zeros((rows, 128), F32)), own_lane_w)
 
     with jax.named_scope("far2"):
         far2()
@@ -277,6 +304,7 @@
         sum2()
 
     with jax.named_scope("early"):
+        wait_bytes(eight, near_recv.at[3])
         for axis in (0, 1):
             both = first_axis(axis, 3)
             if axis == 0:
@@ -326,7 +354,7 @@
 
                 acc = lax.fori_loop(0, part // step, one, acc)
 
-    vec = by_layer(acc, 0) + w_sum
+    vec = by_layer(acc, own_lane) + w_sum
     sums[0] = vec
     got[me] = vec
 
@@ -340,18 +368,19 @@
             device_id_type=MESH,
         ).start()
 
+    far_from = (0, 1, 2, 1)
+    away = sorted(
+        ((ds, dy, dx, c) for ds in range(n_section) for dy in range(SIDE) for dx in range(SIDE) for c in (0, 1)),
+        key=lambda a: -sum(far_from[k] for k in a[:3]) - a[3] / 2,
+    )
     sections = [lax.rem(section + k, n_section) for k in range(n_section)]
-
-    def tell_shard(k, _):
-        to_shard = lax.rem(shard + k, n_shard)
-        for to_section in sections:
-            tell(to_section, to_shard)
-        return 0
-
+    shards_at = {
+        (dy, dx, c): chip_at(dy, dx) * 2 + (core if c == 0 else 1 - core)
+        for dy in range(SIDE) for dx in range(SIDE) for c in (0, 1)
+    }
     with jax.named_scope("tell"):
-        lax.fori_loop(1, n_shard, tell_shard, 0)
-        for to_section in sections[1:]:
-            tell(to_section, shard)
+        for ds, dy, dx, c in away[:-1]:
+            tell(sections[ds], shards_at[dy, dx, c])
     n_all = n_section * n_shard
     others = got.at[pl.ds(0, n_all - 1)]
     with jax.named_scope("everyone"):
@@ -365,11 +394,8 @@
     ratios = jnp.sqrt(pltpu.roll(wide, 120, 1) / (wide + 1.0))[0:1]
     ratios = jnp.where(lane < 8, ratios, 0.0)
     out_ratios[...] = ratios
-    scale = []
-    for b in range(blocks):
-        r = jnp.sum(jnp.where(lane == layers[b], ratios, 0.0), keepdims=True)
-        scale.append(jnp.where(lives[b] > 0, 0.1 * r, 0.0))
-    out_scale[...] = per_row(scale)
+    row_ratio = jnp.sum(jnp.where(own_lane, ratios, 0.0), axis=1, keepdims=True)
+    out_scale[...] = jnp.broadcast_to(0.1 * row_ratio, (rows, 128))
 
     with jax.named_scope("drain"):
         wait_bytes(theirs, pair_send)
@@ -378,18 +404,20 @@
         wait_bytes(others, sum_send)
 
 
-def finish(upd, first, second, weights, scale, ratios, out_params, out_first, out_second, out_ratios, stage, sem):
+def finish(upd, first, second, weights, scale, ratios, out_params, out_first, out_second, out_ratios, stage, ratio, sem):
     columns = stage.shape[1]
     step = columns // 4
     copies = [
         pltpu.make_async_copy(first, out_first, sem.at[0]),
         pltpu.make_async_copy(second, out_second, sem.at[1]),
     ]
+    ratio[...] = ratios[:, : ratio.shape[1]]
+    copies.append(pltpu.make_async_copy(ratio, out_ratios, sem.at[6]))
     for c in copies:
         c.start()
-    out_ratios[...] = ratios[:, : out_ratios.shape[1]]
     row_scale = scale[...]
     for n in range(4):
+      with jax.named_scope(f"fin{n}"):
 
         def one(i, _, n=n):
             for k in range(4):
@@ -403,11 +431,13 @@
         c = pltpu.make_async_copy(stage.at[:, cols], out_params.at[0, :, cols], sem.at[2 + n])
         c.start()
         copies.append(c)
-    for c in copies:
+    with jax.named_scope("finw"):
+      for c in copies:
         c.wait()
 
 
 PARTS = 4
+PARTS0 = 4
 
 
 def shards(grad_parts, params, moment_first, moment_second, block_layer, block_valid, decay):
@@ -417,7 +447,7 @@
     chips = SIDE * SIDE
     hbm, vmem = pl.BlockSpec(memory_space=pltpu.HBM), pl.BlockSpec(memory_space=pltpu.VMEM)
     dma = pltpu.SemaphoreType.DMA
-    groups = 9
+    groups = 8
     upd, first, second, weights, scale, ratios = pl.pallas_call(
         functools.partial(kernel, n_section, n_shard),
         out_shape=(
@@ -443,15 +473,17 @@
             pltpu.VMEM((n_section * n_shard, 1, 128), F32),
             dma((groups,)),
             dma,
-            dma((groups,)),
             dma,
             dma((4,)),
-            dma((2, 4)),
+            dma((4,)),
             dma,
             dma,
             dma((PARTS,)),
             dma,
-            dma((8,)),
+            dma((PARTS0,)),
+            dma,
+            dma((3,)),
+            dma((2,)),
             dma,
             dma,
         ],
@@ -472,8 +504,8 @@
             jax.ShapeDtypeStruct((1, decay.shape[0]), F32),
         ),
         in_specs=[vmem] * 6,
-        out_specs=(hbm, hbm, hbm, vmem),
-        scratch_shapes=[pltpu.VMEM((rows, columns), BF16), dma((6,))],
+        out_specs=(hbm,) * 4,
+        scratch_shapes=[pltpu.VMEM((rows, columns), BF16), pltpu.VMEM((1, decay.shape[0]), F32), dma((7,))],
         compiler_params=pltpu.CompilerParams(vmem_limit_bytes=8 * 2**20),
         name="finish",
     )(upd, first, second, weights, scale, ratios)

time: 63.2 us -> 61.8 us (0.978)
  Pallas kernels: 62.4 us -> 61 us
    pallas_call x1, Pallas kernels: 60.4 us -> 59.5 us  [shards(): pl.pallas_call(functools.partial(kernel, n_section, n_shard), out_shape=(...]
where the time goes in v3:
time: 61.8 us; the launch traced here: 61.6 us
  Pallas kernels  61 us (99%)
  between operations  0.64 us (1%)
    pallas_call x1, Pallas kernels, shards(): pl.pallas_call(functools.partial(kernel, n_section, n_shard), out_shape=(...  59.5 us
    pallas_call x1, Pallas kernels, shards(): pl.pallas_call(finish, out_shape=(jax.ShapeDtypeStruct(params.shape, para...  1.54 us

profile of v3, /device:TPU:1, one launch (start us, length us, event | category | flops | bytes accessed | tf_op | source)
XLA Modules:
  0.0 61.6 jit_solution(11103537752898146507)
XLA Ops:
  0.6 59.5 %lamb_step.1 = (f32[1,32,8192]{2,1,0:T(8,128)S(1)}, f32[1,32,8192]{2,1,0:T(8,128)S(1)}, f32[1,32,8192]{2,1,0:T(8,128)S(1)}, bf16[1,32,8192]{2,1,0:T(8,128)(2,1)S...) custom-call(bf16[1,1,1024,8192]{3,2,1,0:T(8,128)(2,1)} %grads.1, bf16[1,32,8192]{2,1,0:T(8,128)(2,1)} %params.1, ...), custom_call_target="tpu_custom_call" | custom-call | tf_op jit(solution)/shard_map/lamb_step/pallas_call | solution.py:451
  60.1 1.5 %finish.1 = (bf16[1,32,8192]{2,1,0:T(8,128)(2,1)}, f32[1,32,8192]{2,1,0:T(8,128)}, f32[1,32,8192]{2,1,0:T(8,128)}, f32[1,8]{1,0:T(1,128)}) custom-call(f32[1,32,8192]{2,1,0:T(8,128)S(1)} %get-tuple-element.14.upd, f32[1,32,8192]{2,1,0:T(8,128)S(1)} %get-tuple-element.15.first, f32[1,32,8192]{2,1,0:T(8,128)S(1)} %get-tuple-element.16.second, ...), custom_call_target="tpu_custom_call" | custom-call | tf_op jit(solution)/shard_map/finish/pallas_call | solution.py:498

commit v4 on v3

--- a/solution.py
+++ b/solution.py
@@ -26,16 +26,15 @@
 def kernel(
     n_section, n_shard,
     grads, params, m_first, m_second, layer_hbm, valid_hbm, decay_hbm,
-    upd, f_buf, s_buf, w_buf, out_scale, out_ratios,
-    mine, theirs, ahead, landed, late, layer, valid, decay, sums, got,
+    upd, f_buf, s_buf, w_buf, out_mask, got,
+    mine, theirs, ahead, landed, late, layer, valid, decay, sums,
     here_sem, pair_send, link_send, far_recv, near_recv, far2_recv, own2_recv, sum2_recv, sum2_send,
     start_recv, ahead_sem, small_sem, io_sem, sum_send, sum_recv,
 ):
     rows = w_buf.shape[1]
     columns = w_buf.shape[2]
     width = landed.shape[3]
-    part = late.shape[3]
-    parts = width // part
+    parts = [(sum(PARTS[:p]) * (width // 16), PARTS[p] * (width // 16)) for p in range(len(PARTS))]
     section, shard = lax.axis_index("section"), lax.axis_index("shard")
     core, x, y = lax.rem(shard, 2), lax.rem(lax.div(shard, 2), SIDE), lax.div(shard, 2 * SIDE)
     me = section * n_shard + shard
@@ -180,7 +179,7 @@
     def far_first():
         wait_bytes(mine.at[0, pl.ds(0, 2)], here_sem.at[0])
         for p in range(PARTS0):
-            wait_bytes(late.at[pl.ds(0, PARTS // PARTS0)], start_recv.at[p])
+            wait_bytes(ahead.at[0, :, pl.ds(0, 4 * size0)], start_recv.at[p])
             for axis, d, link in each:
                 here = pl.ds(p * size0, size0)
                 terms = [t.at[:, here] for t in own_terms(axis, block_at(axis, 2, 2), d)]
@@ -237,13 +236,13 @@
 
     def sum2():
         wait_bytes(four, far2_recv)
-        for p in range(parts):
+        for p, (start, size) in enumerate(parts):
             for axis, d, _ in each:
                 link = 2 * (1 - axis) + d
-                at = pl.ds(p * part, part)
+                at = pl.ds(start, size)
                 dst = quarter(mine, axis, block_at(axis, 0, signs[d]), d).at[:, at]
                 add_up(dst, [dst, landed.at[link, FAR2].at[:, at]])
-                send(link, dst, late.at[p, link], sum2_recv.at[p], sum2_send)
+                send(link, dst, late.at[link, :, at], sum2_recv.at[p], sum2_send)
 
     with jax.named_scope("far0"):
         far_first()
@@ -261,7 +260,6 @@
         c.wait()
     wait_bytes(theirs.at[0, pl.ds(0, 8)], io_sem.at[1])
     row_block = lax.broadcasted_iota(jnp.int32, (rows, 128), 0) // 8
-    lane = lax.broadcasted_iota(jnp.int32, (1, 128), 1)
     blocks = rows // 8
 
     def per_row(values):
@@ -279,6 +277,7 @@
     row_lane = lax.broadcasted_iota(jnp.int32, (rows, 128), 1)
     own_lane = (row_lane == row_layer) & row_live
     own_lane_w = (row_lane == row_layer + 8) & row_live
+    out_mask[...] = jnp.where(own_lane, 1.0, 0.0)
 
     def by_layer(total, lanes):
         in_row = jnp.sum(total, axis=1, keepdims=True)
@@ -325,13 +324,13 @@
                 lax.fori_loop(0, width // min(512, width), before, 0)
 
     acc = jnp.zeros((rows, 128), F32)
-    for p in range(parts):
+    for p, (start, part) in enumerate(parts):
         with jax.named_scope(f"late{p}"):
-            wait_bytes(late.at[p], sum2_recv.at[p])
+            wait_bytes(late.at[:, :, pl.ds(start, part)], sum2_recv.at[p])
         for axis in (0, 1):
             for q in (0, 1):
-                came = late.at[p, 2 * (1 - axis) + q]
-                base = (2 * axis + q) * width + p * part
+                came = late.at[2 * (1 - axis) + q, :, pl.ds(start, part)]
+                base = (2 * axis + q) * width + start
                 step = min(512, part)
 
                 def one(i, acc, came=came, base=base, step=step):
@@ -386,17 +385,6 @@
     with jax.named_scope("everyone"):
         wait_bytes(others, sum_recv)
 
-    def add_device(k, t):
-        return t + got[k]
-
-    total = lax.fori_loop(0, n_all, add_device, jnp.zeros((1, 128), F32), unroll=8)
-    wide = jnp.broadcast_to(total, (8, 128))
-    ratios = jnp.sqrt(pltpu.roll(wide, 120, 1) / (wide + 1.0))[0:1]
-    ratios = jnp.where(lane < 8, ratios, 0.0)
-    out_ratios[...] = ratios
-    row_ratio = jnp.sum(jnp.where(own_lane, ratios, 0.0), axis=1, keepdims=True)
-    out_scale[...] = jnp.broadcast_to(0.1 * row_ratio, (rows, 128))
-
     with jax.named_scope("drain"):
         wait_bytes(theirs, pair_send)
         wait_bytes(landed, link_send)
@@ -404,18 +392,30 @@
         wait_bytes(others, sum_send)
 
 
-def finish(upd, first, second, weights, scale, ratios, out_params, out_first, out_second, out_ratios, stage, ratio, sem):
+def finish(upd, first, second, weights, mask, got, out_params, out_first, out_second, out_ratios, stage, ratio, sem):
     columns = stage.shape[1]
     step = columns // 4
     copies = [
         pltpu.make_async_copy(first, out_first, sem.at[0]),
         pltpu.make_async_copy(second, out_second, sem.at[1]),
     ]
-    ratio[...] = ratios[:, : ratio.shape[1]]
-    copies.append(pltpu.make_async_copy(ratio, out_ratios, sem.at[6]))
     for c in copies:
         c.start()
-    row_scale = scale[...]
+    several = [got[k] for k in range(8)]
+    for k in range(8, got.shape[0]):
+        several[k % 8] = several[k % 8] + got[k]
+    while len(several) > 1:
+        several = [a + b for a, b in zip(several[::2], several[1::2])]
+    wide = jnp.broadcast_to(several[0], (8, 128))
+    lane = lax.broadcasted_iota(jnp.int32, (1, 128), 1)
+    ratios = jnp.sqrt(pltpu.roll(wide, 120, 1) / (wide + 1.0))[0:1]
+    ratios = jnp.where(lane < ratio.shape[1], ratios, 0.0)
+    ratio[...] = ratios[:, : ratio.shape[1]]
+    c = pltpu.make_async_copy(ratio, out_ratios, sem.at[6])
+    c.start()
+    copies.append(c)
+    row_ratio = jnp.sum(jnp.where(mask[...] > 0.5, ratios, 0.0), axis=1, keepdims=True)
+    row_scale = jnp.broadcast_to(0.1 * row_ratio, mask.shape)
     for n in range(4):
       with jax.named_scope(f"fin{n}"):
 
@@ -436,7 +436,7 @@
         c.wait()
 
 
-PARTS = 4
+PARTS = (8, 4, 2, 2)
 PARTS0 = 4
 
 
@@ -448,7 +448,7 @@
     hbm, vmem = pl.BlockSpec(memory_space=pltpu.HBM), pl.BlockSpec(memory_space=pltpu.VMEM)
     dma = pltpu.SemaphoreType.DMA
     groups = 8
-    upd, first, second, weights, scale, ratios = pl.pallas_call(
+    upd, first, second, weights, mask, got = pl.pallas_call(
         functools.partial(kernel, n_section, n_shard),
         out_shape=(
             pltpu.VMEM(moment_first.shape, F32),
@@ -456,7 +456,7 @@
             pltpu.VMEM(moment_first.shape, F32),
             pltpu.VMEM(params.shape, BF16),
             pltpu.VMEM((rows, 128), F32),
-            pltpu.VMEM((1, 128), F32),
+            pltpu.VMEM((n_section * n_shard, 1, 128), F32),
         ),
         in_specs=[hbm] * 7,
         out_specs=(vmem,) * 6,
@@ -465,12 +465,11 @@
             pltpu.VMEM((2, chips, rows, 2 * width), BF16),
             pltpu.VMEM((2, rows, 2 * width), BF16),
             pltpu.VMEM((4, SLOTS, rows, width), BF16),
-            pltpu.VMEM((PARTS, 4, rows, width // PARTS), BF16),
+            pltpu.VMEM((4, rows, width), BF16),
             pltpu.SMEM(block_layer.shape, jnp.int32),
             pltpu.SMEM(block_valid.shape, jnp.int32),
             pltpu.SMEM(decay.shape, F32),
             pltpu.VMEM((1, 1, 128), F32),
-            pltpu.VMEM((n_section * n_shard, 1, 128), F32),
             dma((groups,)),
             dma,
             dma,
@@ -478,7 +477,7 @@
             dma((4,)),
             dma,
             dma,
-            dma((PARTS,)),
+            dma((len(PARTS),)),
             dma,
             dma((PARTS0,)),
             dma,
@@ -508,7 +507,7 @@
         scratch_shapes=[pltpu.VMEM((rows, columns), BF16), pltpu.VMEM((1, decay.shape[0]), F32), dma((7,))],
         compiler_params=pltpu.CompilerParams(vmem_limit_bytes=8 * 2**20),
         name="finish",
-    )(upd, first, second, weights, scale, ratios)
+    )(upd, first, second, weights, mask, got)
     return new_params, new_first, new_second, ratios[0]
 
 

time: 61.8 us -> 61.4 us (level)
  no operation moved by 1% of the time
where the time goes in v4:
time: 61.4 us; the launch traced here: 61.3 us
  Pallas kernels  60.7 us (99%)
  between operations  0.64 us (1%)
    pallas_call x1, Pallas kernels, shards(): pl.pallas_call(functools.partial(kernel, n_section, n_shard), out_shape=(...  59.1 us
    pallas_call x1, Pallas kernels, shards(): pl.pallas_call(finish, out_shape=(jax.ShapeDtypeStruct(params.shape, para...  1.56 us

profile of v4, /device:TPU:1, one launch (start us, length us, event | category | flops | bytes accessed | tf_op | source)
XLA Modules:
  0.0 61.3 jit_solution(2207506232697864951)
XLA Ops:
  0.6 59.1 %lamb_step.1 = (f32[1,32,8192]{2,1,0:T(8,128)S(1)}, f32[1,32,8192]{2,1,0:T(8,128)S(1)}, f32[1,32,8192]{2,1,0:T(8,128)S(1)}, bf16[1,32,8192]{2,1,0:T(8,128)(2,1)S...) custom-call(bf16[1,1,1024,8192]{3,2,1,0:T(8,128)(2,1)} %grads.1, bf16[1,32,8192]{2,1,0:T(8,128)(2,1)} %params.1, ...), custom_call_target="tpu_custom_call" | custom-call | tf_op jit(solution)/shard_map/lamb_step/pallas_call | solution.py:451
  59.7 1.6 %finish.1 = (bf16[1,32,8192]{2,1,0:T(8,128)(2,1)}, f32[1,32,8192]{2,1,0:T(8,128)}, f32[1,32,8192]{2,1,0:T(8,128)}, f32[1,8]{1,0:T(1,128)}) custom-call(f32[1,32,8192]{2,1,0:T(8,128)S(1)} %get-tuple-element.14.upd, f32[1,32,8192]{2,1,0:T(8,128)S(1)} %get-tuple-element.15.first, f32[1,32,8192]{2,1,0:T(8,128)S(1)} %get-tuple-element.16.second, ...), custom_call_target="tpu_custom_call" | custom-call | tf_op jit(solution)/shard_map/finish/pallas_call | solution.py:497

commit v5 on v4

--- a/solution.py
+++ b/solution.py
@@ -28,8 +28,8 @@
     grads, params, m_first, m_second, layer_hbm, valid_hbm, decay_hbm,
     upd, f_buf, s_buf, w_buf, out_mask, got,
     mine, theirs, ahead, landed, late, layer, valid, decay, sums,
-    here_sem, pair_send, link_send, far_recv, near_recv, far2_recv, own2_recv, sum2_recv, sum2_send,
-    start_recv, ahead_sem, small_sem, io_sem, sum_send, sum_recv,
+    here_sem, pair_send, link_send, far_recv, near_recv, far2_recv, own2_recv, own2_send, sum2_recv, sum2_send,
+    start_recv, heard, near_in, roots_in, all_in, go_on, ahead_sem, small_sem, io_sem, sum_send, sum_recv,
 ):
     rows = w_buf.shape[1]
     columns = w_buf.shape[2]
@@ -45,13 +45,49 @@
 
     links = tuple(chip_at(dy, dx) * 2 + core for dy, dx in ((0, 1), (0, 3), (1, 0), (3, 0)))
 
+    root = (core == 1) & (x == 0) & (y == 0)
+
+    def to_shards(sem, peers):
+        for peer in peers:
+            pl.semaphore_signal(sem, inc=1, device_id={"shard": peer}, device_id_type=MESH)
+
+    def to_roots(sem):
+        for k in range(1, n_section):
+            pl.semaphore_signal(
+                sem, inc=1, device_id={"section": lax.rem(section + k, n_section)}, device_id_type=MESH
+            )
+
     barrier = pltpu.get_barrier_semaphore()
-    for peer in (partner,) + links:
-        pl.semaphore_signal(barrier, inc=1, device_id={"shard": peer}, device_id_type=MESH)
-    for k in range(1, n_section):
-        pl.semaphore_signal(
-            barrier, inc=1, device_id={"section": lax.rem(section + k, n_section)}, device_id_type=MESH
-        )
+    to_shards(barrier, (partner,))
+
+    @pl.when(core == 1)
+    def _():
+        to_shards(barrier, links)
+
+    @pl.when(root)
+    def _():
+        to_roots(barrier)
+
+    def hear(k):
+        @pl.when(core == 1)
+        def _():
+            pl.semaphore_wait(heard.at[k], len(links))
+            if k + 1 < ROUNDS:
+                to_shards(heard.at[k + 1], links)
+            if k == 0:
+                to_shards(near_in, (partner,))
+
+        if k + 1 == ROUNDS:
+
+            @pl.when(root)
+            def _():
+                to_roots(roots_in)
+
+    def hear_roots():
+        @pl.when(root)
+        def _():
+            pl.semaphore_wait(roots_in, n_section - 1)
+            to_shards(all_in, [k for k in range(n_shard) if k != 1])
 
     groups = []
     for j in ORDER:
@@ -60,6 +96,9 @@
         groups.append([(h, block_at(h, main, j)) for main in (1, 3, 0) for h in (0, 1)])
     group_of = {b: g for g, blocks in enumerate(groups) for b in blocks}
 
+    size0 = width // PARTS0
+    first4 = [(h, q) for h in (0, 1) for q in (0, 1)]
+
     def source(h, block, which):
         chip = chip_at(block // SIDE, block % SIDE)
         at = pl.multiple_of(chip * (2 * rows) + which * rows, rows)
@@ -70,8 +109,11 @@
             source(h, block, core), mine.at[h, block], here_sem.at[group_of[h, block]]
         )
 
-    def fetch_ahead(h):
-        return pltpu.make_async_copy(source(h, block_at(h, 2, 2), 1 - core), ahead.at[h], ahead_sem)
+    def fetch_ahead(p, h, q):
+        cols = pl.ds(q * width + p * size0, size0)
+        return pltpu.make_async_copy(
+            source(h, block_at(h, 2, 2), 1 - core).at[:, cols], ahead.at[h, :, cols], ahead_sem.at[p]
+        )
 
     def pair(h, block):
         return pltpu.make_async_remote_copy(
@@ -82,8 +124,6 @@
             device_id={"shard": partner},
             device_id_type=MESH,
         )
-
-    size0 = width // PARTS0
 
     def pair0(p, h, q):
         cols = pl.ds(q * width + p * size0, size0)
@@ -115,6 +155,7 @@
     def add_up(dst, terms):
         size = dst.shape[1]
         step = min(512, size)
+        assert size % step == 0
 
         def one(i, _):
             cols = pl.ds(pl.multiple_of(i * step, step), step)
@@ -129,18 +170,35 @@
 
         lax.fori_loop(0, size // step, one, 0)
 
-    for h in (0, 1):
-        fetch_ahead(h).start()
-        load(h, block_at(h, 2, 2)).start()
+    for p in range(PARTS0):
+        for h, q in first4:
+            fetch_ahead(p, h, q).start()
+        if p == 0:
+            for h in (0, 1):
+                load(h, block_at(h, 2, 2)).start()
     for h, block in groups[1]:
         load(h, block).start()
     with jax.named_scope("barrier"):
-        pl.semaphore_wait(barrier, 1 + len(links) + n_section - 1)
-    wait_bytes(ahead, ahead_sem)
+        @pl.when(core == 0)
+        def _():
+            pl.semaphore_wait(barrier, 1)
+
+        @pl.when((core == 1) & jnp.logical_not(root))
+        def _():
+            pl.semaphore_wait(barrier, 1 + len(links))
+
+        @pl.when(root)
+        def _():
+            pl.semaphore_wait(barrier, 1 + len(links) + n_section - 1)
+
+        @pl.when(core == 1)
+        def _():
+            to_shards(heard.at[0], links)
+
     for p in range(PARTS0):
-        for h in (0, 1):
-            for q in (0, 1):
-                pair0(p, h, q).start()
+        wait_bytes(ahead.at[0, :, pl.ds(0, 4 * size0)], ahead_sem.at[p])
+        for h, q in first4:
+            pair0(p, h, q).start()
     small = [
         pltpu.make_async_copy(a, b, small_sem.at[k])
         for k, (a, b) in enumerate(((layer_hbm, layer), (valid_hbm, valid), (decay_hbm, decay)))
@@ -180,11 +238,19 @@
         wait_bytes(mine.at[0, pl.ds(0, 2)], here_sem.at[0])
         for p in range(PARTS0):
             wait_bytes(ahead.at[0, :, pl.ds(0, 4 * size0)], start_recv.at[p])
+            if p == 0:
+
+                @pl.when(core == 0)
+                def _():
+                    pl.semaphore_wait(near_in, 1)
+
             for axis, d, link in each:
                 here = pl.ds(p * size0, size0)
                 terms = [t.at[:, here] for t in own_terms(axis, block_at(axis, 2, 2), d)]
                 add_up(terms[0], terms)
                 send(link, terms[0], landed.at[link, FAR[0], :, here], far_recv.at[0])
+            if p == 0:
+                hear(0)
 
     def far(j):
         for axis, d, link in each:
@@ -232,11 +298,17 @@
         for axis, d, _ in each:
             link = 2 * (1 - axis) + d
             src = quarter(mine, axis, block_at(axis, 0, signs[d]), 1 - d)
-            send(link, src, landed.at[link, OWN2], own2_recv)
+            send(link, src, landed.at[link, OWN2], own2_recv, own2_send)
 
     def sum2():
         wait_bytes(four, far2_recv)
+
         for p, (start, size) in enumerate(parts):
+            if p == 1:
+                @pl.when(core == 1)
+                def _():
+                    pl.semaphore_wait(go_on, 1)
+
             for axis, d, _ in each:
                 link = 2 * (1 - axis) + d
                 at = pl.ds(start, size)
@@ -249,12 +321,20 @@
     for j in range(1, 4):
         with jax.named_scope(f"far{j}"):
             far(j)
+        hear(j)
     for j in range(3):
         with jax.named_scope(f"own{j}"):
             near_own(j)
         with jax.named_scope(f"sum{j}"):
             near_sum(j)
+        if j == 1:
+            hear_roots()
     near_own(3)
+
+    @pl.when(jnp.logical_not(root))
+    def _():
+        pl.semaphore_wait(all_in, 1)
+
 
     for c in small + io[:1]:
         c.wait()
@@ -301,6 +381,13 @@
         own2()
     with jax.named_scope("sum2"):
         sum2()
+
+    with jax.named_scope("own2_sent"):
+        wait_bytes(four, own2_send)
+
+        @pl.when(core == 0)
+        def _():
+            to_shards(go_on, (partner,))
 
     with jax.named_scope("early"):
         wait_bytes(eight, near_recv.at[3])
@@ -332,6 +419,7 @@
                 came = late.at[2 * (1 - axis) + q, :, pl.ds(start, part)]
                 base = (2 * axis + q) * width + start
                 step = min(512, part)
+                assert part % step == 0
 
                 def one(i, acc, came=came, base=base, step=step):
                     for k in range(step // 128):
@@ -387,7 +475,7 @@
 
     with jax.named_scope("drain"):
         wait_bytes(theirs, pair_send)
-        wait_bytes(landed, link_send)
+        wait_bytes(landed.at[:, pl.ds(0, SLOTS - 1)], link_send)
         wait_bytes(late, sum2_send)
         wait_bytes(others, sum_send)
 
@@ -436,8 +524,9 @@
         c.wait()
 
 
-PARTS = (8, 4, 2, 2)
+PARTS = (4, 4, 4, 2, 2)
 PARTS0 = 4
+ROUNDS = 4
 
 
 def shards(grad_parts, params, moment_first, moment_second, block_layer, block_valid, decay):
@@ -477,10 +566,16 @@
             dma((4,)),
             dma,
             dma,
+            dma,
             dma((len(PARTS),)),
             dma,
             dma((PARTS0,)),
-            dma,
+            pltpu.SemaphoreType.REGULAR((ROUNDS,)),
+            pltpu.SemaphoreType.REGULAR,
+            pltpu.SemaphoreType.REGULAR,
+            pltpu.SemaphoreType.REGULAR,
+            pltpu.SemaphoreType.REGULAR,
+            dma((PARTS0,)),
             dma((3,)),
             dma((2,)),
             dma,

time: 61.4 us -> 60.5 us (0.985)
  Pallas kernels: 60.7 us -> 59.8 us
    pallas_call x1, Pallas kernels: 59.1 us -> 58.2 us  [shards(): pl.pallas_call(functools.partial(kernel, n_section, n_shard), out_shape=(...]
where the time goes in v5:
time: 60.5 us; the launch traced here: 60.4 us
  Pallas kernels  59.8 us (99%)
  between operations  0.64 us (1%)
    pallas_call x1, Pallas kernels, shards(): pl.pallas_call(functools.partial(kernel, n_section, n_shard), out_shape=(...  58.2 us
    pallas_call x1, Pallas kernels, shards(): pl.pallas_call(finish, out_shape=(jax.ShapeDtypeStruct(params.shape, para...  1.56 us

profile of v5, /device:TPU:1, one launch (start us, length us, event | category | flops | bytes accessed | tf_op | source)
XLA Modules:
  0.0 60.4 jit_solution(1570907430855801682)
XLA Ops:
  0.6 58.2 %lamb_step.1 = (f32[1,32,8192]{2,1,0:T(8,128)S(1)}, f32[1,32,8192]{2,1,0:T(8,128)S(1)}, f32[1,32,8192]{2,1,0:T(8,128)S(1)}, bf16[1,32,8192]{2,1,0:T(8,128)(2,1)S...) custom-call(bf16[1,1,1024,8192]{3,2,1,0:T(8,128)(2,1)} %grads.1, bf16[1,32,8192]{2,1,0:T(8,128)(2,1)} %params.1, ...), custom_call_target="tpu_custom_call" | custom-call | tf_op jit(solution)/shard_map/lamb_step/pallas_call | solution.py:540
  58.8 1.6 %finish.1 = (bf16[1,32,8192]{2,1,0:T(8,128)(2,1)}, f32[1,32,8192]{2,1,0:T(8,128)}, f32[1,32,8192]{2,1,0:T(8,128)}, f32[1,8]{1,0:T(1,128)}) custom-call(f32[1,32,8192]{2,1,0:T(8,128)S(1)} %get-tuple-element.14.upd, f32[1,32,8192]{2,1,0:T(8,128)S(1)} %get-tuple-element.15.first, f32[1,32,8192]{2,1,0:T(8,128)S(1)} %get-tuple-element.16.second, ...), custom_call_target="tpu_custom_call" | custom-call | tf_op jit(solution)/shard_map/finish/pallas_call | solution.py:592

commit v6 on v5

--- a/solution.py
+++ b/solution.py
@@ -27,9 +27,9 @@
     n_section, n_shard,
     grads, params, m_first, m_second, layer_hbm, valid_hbm, decay_hbm,
     upd, f_buf, s_buf, w_buf, out_mask, got,
-    mine, theirs, ahead, landed, late, layer, valid, decay, sums,
+    mine, theirs, landed, late, layer, valid, decay, sums,
     here_sem, pair_send, link_send, far_recv, near_recv, far2_recv, own2_recv, own2_send, sum2_recv, sum2_send,
-    start_recv, heard, near_in, roots_in, all_in, go_on, ahead_sem, small_sem, io_sem, sum_send, sum_recv,
+    start_recv, heard, near_in, roots_in, all_in, go_on, small_sem, io_sem, sum_send, sum_recv,
 ):
     rows = w_buf.shape[1]
     columns = w_buf.shape[2]
@@ -109,6 +109,11 @@
             source(h, block, core), mine.at[h, block], here_sem.at[group_of[h, block]]
         )
 
+    def load(h, block):
+        return pltpu.make_async_copy(
+            source(h, block, core), mine.at[h, block], here_sem.at[group_of[h, block]]
+        )
+
     def fetch_ahead(p, h, q):
         cols = pl.ds(q * width + p * size0, size0)
         return pltpu.make_async_copy(
@@ -128,7 +133,7 @@
     def pair0(p, h, q):
         cols = pl.ds(q * width + p * size0, size0)
         return pltpu.make_async_remote_copy(
-            src_ref=ahead.at[h, :, cols],
+            src_ref=source(h, block_at(h, 2, 2), 1 - core).at[:, cols],
             dst_ref=theirs.at[h, block_at(h, 2, 2), :, cols],
             send_sem=pair_send,
             recv_sem=start_recv.at[p],
@@ -170,13 +175,7 @@
 
         lax.fori_loop(0, size // step, one, 0)
 
-    for p in range(PARTS0):
-        for h, q in first4:
-            fetch_ahead(p, h, q).start()
-        if p == 0:
-            for h in (0, 1):
-                load(h, block_at(h, 2, 2)).start()
-    for h, block in groups[1]:
+    for h, block in groups[0] + groups[1]:
         load(h, block).start()
     with jax.named_scope("barrier"):
         @pl.when(core == 0)
@@ -196,7 +195,6 @@
             to_shards(heard.at[0], links)
 
     for p in range(PARTS0):
-        wait_bytes(ahead.at[0, :, pl.ds(0, 4 * size0)], ahead_sem.at[p])
         for h, q in first4:
             pair0(p, h, q).start()
     small = [
@@ -237,7 +235,7 @@
     def far_first():
         wait_bytes(mine.at[0, pl.ds(0, 2)], here_sem.at[0])
         for p in range(PARTS0):
-            wait_bytes(ahead.at[0, :, pl.ds(0, 4 * size0)], start_recv.at[p])
+            wait_bytes(landed.at[0, 0, :, pl.ds(0, 4 * size0)], start_recv.at[p])
             if p == 0:
 
                 @pl.when(core == 0)
@@ -249,8 +247,7 @@
                 terms = [t.at[:, here] for t in own_terms(axis, block_at(axis, 2, 2), d)]
                 add_up(terms[0], terms)
                 send(link, terms[0], landed.at[link, FAR[0], :, here], far_recv.at[0])
-            if p == 0:
-                hear(0)
+        hear(0)
 
     def far(j):
         for axis, d, link in each:
@@ -304,7 +301,7 @@
         wait_bytes(four, far2_recv)
 
         for p, (start, size) in enumerate(parts):
-            if p == 1:
+            if p == 0:
                 @pl.when(core == 1)
                 def _():
                     pl.semaphore_wait(go_on, 1)
@@ -552,7 +549,6 @@
         scratch_shapes=[
             pltpu.VMEM((2, chips, rows, 2 * width), BF16),
             pltpu.VMEM((2, chips, rows, 2 * width), BF16),
-            pltpu.VMEM((2, rows, 2 * width), BF16),
             pltpu.VMEM((4, SLOTS, rows, width), BF16),
             pltpu.VMEM((4, rows, width), BF16),
             pltpu.SMEM(block_layer.shape, jnp.int32),
@@ -575,7 +571,6 @@
             pltpu.SemaphoreType.REGULAR,
             pltpu.SemaphoreType.REGULAR,
             pltpu.SemaphoreType.REGULAR,
-            dma((PARTS0,)),
             dma((3,)),
             dma((2,)),
             dma,

time: 60.5 us -> 59.9 us (0.990)
  Pallas kernels: 59.8 us -> 59.1 us
    pallas_call x1, Pallas kernels: 58.2 us -> 57.6 us  [shards(): pl.pallas_call(functools.partial(kernel, n_section, n_shard), out_shape=(...]
where the time goes in v6:
time: 59.9 us; the launch traced here: 59.8 us
  Pallas kernels  59.1 us (99%)
  between operations  0.64 us (1%)
    pallas_call x1, Pallas kernels, shards(): pl.pallas_call(functools.partial(kernel, n_section, n_shard), out_shape=(...  57.6 us
    pallas_call x1, Pallas kernels, shards(): pl.pallas_call(finish, out_shape=(jax.ShapeDtypeStruct(params.shape, para...  1.56 us

profile of v6, /device:TPU:1, one launch (start us, length us, event | category | flops | bytes accessed | tf_op | source)
XLA Modules:
  0.0 59.8 jit_solution(6896149152292735615)
XLA Ops:
  0.6 57.6 %lamb_step.1 = (f32[1,32,8192]{2,1,0:T(8,128)S(1)}, f32[1,32,8192]{2,1,0:T(8,128)S(1)}, f32[1,32,8192]{2,1,0:T(8,128)S(1)}, bf16[1,32,8192]{2,1,0:T(8,128)(2,1)S...) custom-call(bf16[1,1,1024,8192]{3,2,1,0:T(8,128)(2,1)} %grads.1, bf16[1,32,8192]{2,1,0:T(8,128)(2,1)} %params.1, ...), custom_call_target="tpu_custom_call" | custom-call | tf_op jit(solution)/shard_map/lamb_step/pallas_call | solution.py:537
  58.2 1.6 %finish.1 = (bf16[1,32,8192]{2,1,0:T(8,128)(2,1)}, f32[1,32,8192]{2,1,0:T(8,128)}, f32[1,32,8192]{2,1,0:T(8,128)}, f32[1,8]{1,0:T(1,128)}) custom-call(f32[1,32,8192]{2,1,0:T(8,128)S(1)} %get-tuple-element.14.upd, f32[1,32,8192]{2,1,0:T(8,128)S(1)} %get-tuple-element.15.first, f32[1,32,8192]{2,1,0:T(8,128)S(1)} %get-tuple-element.16.second, ...), custom_call_target="tpu_custom_call" | custom-call | tf_op jit(solution)/shard_map/finish/pallas_call | solution.py:587

commit v7 on v6

--- a/solution.py
+++ b/solution.py
@@ -92,8 +92,8 @@
     groups = []
     for j in ORDER:
         groups.append([(h, block_at(h, 2, j)) for h in (0, 1)])
-    for j in ORDER:
-        groups.append([(h, block_at(h, main, j)) for main in (1, 3, 0) for h in (0, 1)])
+    for some in (ORDER[:1], ORDER[1:2], ORDER[2:]):
+        groups.append([(h, block_at(h, main, j)) for j in some for main in (1, 3, 0) for h in (0, 1)])
     group_of = {b: g for g, blocks in enumerate(groups) for b in blocks}
 
     size0 = width // PARTS0
@@ -222,11 +222,13 @@
         g = group_of[h, block]
         if g not in ready:
             ready.add(g)
-            wait_bytes(mine.at[0, pl.ds(0, 2 * len(groups[g]))], here_sem.at[g])
+            count = 2 * len(groups[g])
+            several = mine.at[0, pl.ds(0, count)] if count <= 16 else mine.at[:, pl.ds(0, count // 2)]
+            wait_bytes(several, here_sem.at[g])
 
     signs = (1, 3)
     each = [(axis, d, 2 * axis + d) for axis in (0, 1) for d in (0, 1)]
-    four, eight = landed.at[0, pl.ds(0, 4)], landed.at[0, pl.ds(0, 8)]
+    four, eight, sixteen = landed.at[0, pl.ds(0, 4)], landed.at[0, pl.ds(0, 8)], landed.at[pl.ds(0, 2), pl.ds(0, 8)]
 
     def own_terms(axis, block, q):
         need(axis, block)
@@ -259,14 +261,14 @@
         for axis, d, link in each:
             terms = own_terms(axis, block_at(axis, signs[d], ORDER[j]), 1 - d)
             add_up(terms[0], terms)
-            send(link, terms[0], landed.at[link, NEAR_OWN[j]], near_recv.at[j])
+            send(link, terms[0], landed.at[link, NEAR_OWN[j]], near_recv.at[(0, 1, 1, 2)[j]])
 
     def near_sum(j):
         wait_bytes(four, far_recv.at[j])
         for axis, d, link in each:
             terms = own_terms(axis, block_at(axis, signs[d], ORDER[j]), d)
             add_up(terms[0], terms + [landed.at[link, FAR[j]]])
-            send(link, terms[0], landed.at[link, NEAR_SUM[j]], near_recv.at[j])
+            send(link, terms[0], landed.at[link, NEAR_SUM[j]], near_recv.at[(0, 1, 1, 2)[j]])
 
     def first_axis(axis, j):
         block = block_at(axis, 0, ORDER[j])
@@ -278,7 +280,8 @@
         ]
 
     def settle(j):
-        wait_bytes(eight, near_recv.at[j])
+        if j != 1:
+            wait_bytes(eight if j == 0 else sixteen, near_recv.at[min(j, 1)])
         for axis in (0, 1):
             for terms in first_axis(axis, j):
                 add_up(terms[0], terms)
@@ -290,8 +293,8 @@
             send(link, quarter(mine, axis, block_at(axis, 0, 2), d), landed.at[link, FAR2], far2_recv)
 
     def own2():
+        settle(2)
         settle(1)
-        settle(2)
         for axis, d, _ in each:
             link = 2 * (1 - axis) + d
             src = quarter(mine, axis, block_at(axis, 0, signs[d]), 1 - d)
@@ -387,7 +390,7 @@
             to_shards(go_on, (partner,))
 
     with jax.named_scope("early"):
-        wait_bytes(eight, near_recv.at[3])
+        wait_bytes(eight, near_recv.at[2])
         for axis in (0, 1):
             both = first_axis(axis, 3)
             if axis == 0:
@@ -533,7 +536,7 @@
     chips = SIDE * SIDE
     hbm, vmem = pl.BlockSpec(memory_space=pltpu.HBM), pl.BlockSpec(memory_space=pltpu.VMEM)
     dma = pltpu.SemaphoreType.DMA
-    groups = 8
+    groups = 7
     upd, first, second, weights, mask, got = pl.pallas_call(
         functools.partial(kernel, n_section, n_shard),
         out_shape=(
@@ -559,7 +562,7 @@
             dma,
             dma,
             dma((4,)),
-            dma((4,)),
+            dma((3,)),
             dma,
             dma,
             dma,

time: 59.9 us -> 59.9 us (level)
  no operation moved by 1% of the time
where the time goes in v7:
time: 59.9 us; the launch traced here: 59.8 us
  Pallas kernels  59.1 us (99%)
  between operations  0.64 us (1%)
    pallas_call x1, Pallas kernels, shards(): pl.pallas_call(functools.partial(kernel, n_section, n_shard), out_shape=(...  57.6 us
    pallas_call x1, Pallas kernels, shards(): pl.pallas_call(finish, out_shape=(jax.ShapeDtypeStruct(params.shape, para...  1.56 us

profile of v7, /device:TPU:1, one launch (start us, length us, event | category | flops | bytes accessed | tf_op | source)
XLA Modules:
  0.0 59.8 jit_solution(11677862643091966008)
XLA Ops:
  0.6 57.6 %lamb_step.1 = (f32[1,32,8192]{2,1,0:T(8,128)S(1)}, f32[1,32,8192]{2,1,0:T(8,128)S(1)}, f32[1,32,8192]{2,1,0:T(8,128)S(1)}, bf16[1,32,8192]{2,1,0:T(8,128)(2,1)S...) custom-call(bf16[1,1,1024,8192]{3,2,1,0:T(8,128)(2,1)} %grads.1, bf16[1,32,8192]{2,1,0:T(8,128)(2,1)} %params.1, ...), custom_call_target="tpu_custom_call" | custom-call | tf_op jit(solution)/shard_map/lamb_step/pallas_call | solution.py:540
  58.2 1.6 %finish.1 = (bf16[1,32,8192]{2,1,0:T(8,128)(2,1)}, f32[1,32,8192]{2,1,0:T(8,128)}, f32[1,32,8192]{2,1,0:T(8,128)}, f32[1,8]{1,0:T(1,128)}) custom-call(f32[1,32,8192]{2,1,0:T(8,128)S(1)} %get-tuple-element.14.upd, f32[1,32,8192]{2,1,0:T(8,128)S(1)} %get-tuple-element.15.first, f32[1,32,8192]{2,1,0:T(8,128)S(1)} %get-tuple-element.16.second, ...), custom_call_target="tpu_custom_call" | custom-call | tf_op jit(solution)/shard_map/finish/pallas_call | solution.py:590

commit v8 on v6

--- a/solution.py
+++ b/solution.py
@@ -175,7 +175,7 @@
 
         lax.fori_loop(0, size // step, one, 0)
 
-    for h, block in groups[0] + groups[1]:
+    for h, block in groups[0]:
         load(h, block).start()
     with jax.named_scope("barrier"):
         @pl.when(core == 0)
@@ -209,9 +209,8 @@
     for g in range(1, len(groups)):
         for h, block in groups[g]:
             pair(h, block).start()
-        if g > 1:
-            for h, block in groups[g]:
-                load(h, block).start()
+        for h, block in groups[g]:
+            load(h, block).start()
         if g == 4:
             for c in small + io:
                 c.start()
@@ -496,7 +495,7 @@
     ratios = jnp.sqrt(pltpu.roll(wide, 120, 1) / (wide + 1.0))[0:1]
     ratios = jnp.where(lane < ratio.shape[1], ratios, 0.0)
     ratio[...] = ratios[:, : ratio.shape[1]]
-    c = pltpu.make_async_copy(ratio, out_ratios, sem.at[6])
+    c = pltpu.make_async_copy(ratio, out_ratios, sem.at[3])
     c.start()
     copies.append(c)
     row_ratio = jnp.sum(jnp.where(mask[...] > 0.5, ratios, 0.0), axis=1, keepdims=True)
@@ -513,12 +512,11 @@
 
         lax.fori_loop(0, step // 512, one, 0)
         cols = pl.ds(n * step, step)
-        c = pltpu.make_async_copy(stage.at[:, cols], out_params.at[0, :, cols], sem.at[2 + n])
-        c.start()
-        copies.append(c)
+        pltpu.make_async_copy(stage.at[:, cols], out_params.at[0, :, cols], sem.at[2]).start()
     with jax.named_scope("finw"):
       for c in copies:
         c.wait()
+      pltpu.make_async_copy(stage, out_params.at[0], sem.at[2]).wait()
 
 
 PARTS = (4, 4, 4, 2, 2)
@@ -594,7 +592,7 @@
         ),
         in_specs=[vmem] * 6,
         out_specs=(hbm,) * 4,
-        scratch_shapes=[pltpu.VMEM((rows, columns), BF16), pltpu.VMEM((1, decay.shape[0]), F32), dma((7,))],
+        scratch_shapes=[pltpu.VMEM((rows, columns), BF16), pltpu.VMEM((1, decay.shape[0]), F32), dma((4,))],
         compiler_params=pltpu.CompilerParams(vmem_limit_bytes=8 * 2**20),
         name="finish",
     )(upd, first, second, weights, mask, got)

time: 59.9 us -> 59.9 us (level)
  no operation moved by 1% of the time
where the time goes in v8:
time: 59.9 us; the launch traced here: 59.7 us
  Pallas kernels  59.1 us (99%)
  between operations  0.64 us (1%)
    pallas_call x1, Pallas kernels, shards(): pl.pallas_call(functools.partial(kernel, n_section, n_shard), out_shape=(...  57.6 us
    pallas_call x1, Pallas kernels, shards(): pl.pallas_call(finish, out_shape=(jax.ShapeDtypeStruct(params.shape, para...  1.54 us

profile of v8, /device:TPU:1, one launch (start us, length us, event | category | flops | bytes accessed | tf_op | source)
XLA Modules:
  0.0 59.7 jit_solution(1632588791432729229)
XLA Ops:
  0.6 57.6 %lamb_step.1 = (f32[1,32,8192]{2,1,0:T(8,128)S(1)}, f32[1,32,8192]{2,1,0:T(8,128)S(1)}, f32[1,32,8192]{2,1,0:T(8,128)S(1)}, bf16[1,32,8192]{2,1,0:T(8,128)(2,1)S...) custom-call(bf16[1,1,1024,8192]{3,2,1,0:T(8,128)(2,1)} %grads.1, bf16[1,32,8192]{2,1,0:T(8,128)(2,1)} %params.1, ...), custom_call_target="tpu_custom_call" | custom-call | tf_op jit(solution)/shard_map/lamb_step/pallas_call | solution.py:535
  58.2 1.5 %finish.1 = (bf16[1,32,8192]{2,1,0:T(8,128)(2,1)}, f32[1,32,8192]{2,1,0:T(8,128)}, f32[1,32,8192]{2,1,0:T(8,128)}, f32[1,8]{1,0:T(1,128)}) custom-call(f32[1,32,8192]{2,1,0:T(8,128)S(1)} %get-tuple-element.14.upd, f32[1,32,8192]{2,1,0:T(8,128)S(1)} %get-tuple-element.15.first, f32[1,32,8192]{2,1,0:T(8,128)S(1)} %get-tuple-element.16.second, ...), custom_call_target="tpu_custom_call" | custom-call | tf_op jit(solution)/shard_map/finish/pallas_call | solution.py:585
